TPU v7x, 128 devices: a whole 4x4x4 slice. The times are simulated.
128 devices in a mesh: batch: 1, outer: 16 (over z, y), rows: 8 (over x, core).
Axes of the slice: x: 4, y: 4, z: 4, core: 2. Of those that a mesh axis runs over, the one named last changes fastest.
Arguments:
- a_mat: float32 [131072, 896], P(('batch', 'outer', 'rows'))
Outputs:
- output 1: float32 [131072, 896], P(('batch', 'outer', 'rows'))
- output 2: float32 [896, 896], P('batch')
All inputs are finite; a program needn't handle non-finite values.
Results may differ from a plain program's by a relative error of at most 0.001.
Values sent between devices are 32-bit elements.
A program may use at most 1 GiB of HBM per device.

v0:
```python
import jax
import jax.numpy as jnp
from jax import lax
from jax.sharding import PartitionSpec as P

FULL_PREC = lax.Precision.HIGHEST
GROUP_AXES = ("outer", "rows")


def sweep_local(row_blk):
    part_gram = lax.dot_general(row_blk, row_blk, (((0,), (0,)), ((), ())), precision=FULL_PREC, preferred_element_type=jnp.float32)
    gram_mat = lax.psum(part_gram, GROUP_AXES)
    low_fac = jnp.linalg.cholesky(gram_mat)
    solved = lax.linalg.triangular_solve(low_fac, row_blk, left_side=False, lower=True, transpose_a=True)
    return solved, low_fac


def solution(mesh):
    row_spec = P(("batch", "outer", "rows"), None)

    def local_qr(row_blk):
        q_one, low_one = sweep_local(row_blk)
        q_two, low_two = sweep_local(q_one)
        r_fac = lax.dot_general(low_two, low_one, (((0,), (1,)), ((), ())), precision=FULL_PREC, preferred_element_type=jnp.float32)
        return q_two, r_fac

    return jax.shard_map(local_qr, mesh=mesh, in_specs=(row_spec,), out_specs=(row_spec, P("batch", None)), check_vma=False)
```

profile of v0, /device:TPU:1, one launch (start us, length us, event | category | flops | bytes accessed | tf_op | source)
XLA Modules:
  0.0 998.7 jit_solution(9425001811965641383)
XLA Ops:
  7.2 15.6 %fusion.156 = f32[896,896]{0,1:T(8,128)} fusion(f32[1024,896]{1,0:T(8,128)} %param.4), kind=kOutput, calls=%fused_computation.283 | convolution fusion | flops 9865003008 | bytes 6881280 | tf_op jit(solution)/shard_map/dot_general | solution.py:11
  22.9 156.4 %all-reduce.4.cloned.1.call-done = f32[896,896]{0,1:T(8,128)} async-done(((f32[896,896]{0,1:T(8,128)}), f32[896,896]{0,1:T(8,128)}) %all-reduce.4.cloned.1.call-update) | async-done | bytes 3211280 | tf_op jit(solution)/shard_map/psum | solution.py:12
  187.9 11.7 %cholesky.536 = f32[128,128]{1,0:T(8,128)S(1)} custom-call(f32[128,128]{1,0:T(8,128)S(1)} %cholesky.790), custom_call_target="Cholesky" | custom-call | tf_op jit(solution)/shard_map/jit(cholesky)/cholesky | solution.py:13
  199.6 9.8 custom-call.48
  213.3 11.7 %cholesky.555 = f32[128,128]{1,0:T(8,128)S(1)} custom-call(f32[128,128]{1,0:T(8,128)S(1)} %cholesky.794), custom_call_target="Cholesky" | custom-call | tf_op jit(solution)/shard_map/jit(cholesky)/cholesky | solution.py:13
  225.1 10.0 %custom-call.49 = f32[1,128,128]{1,2,0:T(8,128)S(1)} custom-call(f32[1,128,128]{2,1,0:T(8,128)S(1)} %get-tuple-element.110), custom_call_target="InvertDiagBlocksLowerTriangular" | custom-call | tf_op jit(solution)/shard_map/jit(cholesky)/cholesky | solution.py:13
  238.8 13.2 %cholesky.576 = f32[128,128]{1,0:T(8,128)} custom-call(f32[128,128]{1,0:T(8,128)} %cholesky.799), custom_call_target="Cholesky" | custom-call | tf_op jit(solution)/shard_map/jit(cholesky)/cholesky | solution.py:13
  254.1 11.3 %custom-call.50 = f32[1,128,128]{1,2,0:T(8,128)} custom-call(f32[1,128,128]{2,1,0:T(8,128)} %get-tuple-element.107), custom_call_target="InvertDiagBlocksLowerTriangular" | custom-call | tf_op jit(solution)/shard_map/jit(cholesky)/cholesky | solution.py:13
  268.3 12.8 %cholesky.595 = f32[128,128]{1,0:T(8,128)} custom-call(f32[128,128]{1,0:T(8,128)S(1)} %cholesky.804), custom_call_target="Cholesky" | custom-call | tf_op jit(solution)/shard_map/jit(cholesky)/cholesky | solution.py:13
  282.7 10.4 %custom-call.51 = f32[1,128,128]{1,2,0:T(8,128)} custom-call(f32[1,128,128]{2,1,0:T(8,128)S(1)} %get-tuple-element.104), custom_call_target="InvertDiagBlocksLowerTriangular" | custom-call | tf_op jit(solution)/shard_map/jit(cholesky)/cholesky | solution.py:13
  296.1 11.7 %cholesky.614 = f32[128,128]{1,0:T(8,128)S(1)} custom-call(f32[128,128]{1,0:T(8,128)S(1)} %cholesky.809), custom_call_target="Cholesky" | custom-call | tf_op jit(solution)/shard_map/jit(cholesky)/cholesky | solution.py:13
  308.4 9.8 custom-call.52
  320.1 11.9 %cholesky.633 = f32[128,128]{1,0:T(8,128)S(1)} custom-call(f32[128,128]{1,0:T(8,128)S(1)} %cholesky.814), custom_call_target="Cholesky" | custom-call | tf_op jit(solution)/shard_map/jit(cholesky)/cholesky | solution.py:13
  344.1 11.7 %cholesky.650 = f32[128,128]{1,0:T(8,128)S(1)} custom-call(f32[128,128]{1,0:T(8,128)S(1)} %convolution_subtract_fusion.19), custom_call_target="Cholesky" | custom-call | tf_op jit(solution)/shard_map/jit(cholesky)/cholesky | solution.py:13
  364.3 24.8 %while.4 = (s32[]{:T(128)}, f32[896,896]{1,0:T(8,128)}, s32[7,2]{0,1:T(2,128)S(1)}, f32[7,128,128]{2,1,0:T(8,128)}, s32[]{:T(128)}) while((s32[]{:T(128)}, f32[896,896]{1,0:T(8,128)}, s32[7,2]{0,1:T(2,128)S(1)}, f32[7,128,128]{2,1,0:T(8,128)}, s32[]{:T(128)}) %tuple.101), condition=%wide.while_cond, body=%wide.while_body.sunk | while | flops 2 | bytes 132205 | solution.py:14
  389.1 70.6 %custom-call.54 = f32[7,128,128]{1,2,0:T(8,128)} custom-call(f32[7,128,128]{2,1,0:T(8,128)} %get-tuple-element.18), custom_call_target="InvertDiagBlocksLowerTriangular" | custom-call | tf_op jit(solution)/shard_map/triangular_solve/custom-call.6 | solution.py:14
  493.7 13.7 %fusion.157 = f32[896,896]{0,1:T(8,128)} fusion(f32[1024,896]{0,1:T(8,128)S(1)} %get-tuple-element.122), kind=kOutput, calls=%fused_computation.284 | convolution fusion | flops 9865003008 | bytes 6881280 | tf_op jit(solution)/shard_map/dot_general | solution.py:11
  507.4 151.6 %all-reduce.6.cloned.1.call-done = f32[896,896]{0,1:T(8,128)} async-done(((f32[896,896]{0,1:T(8,128)}), f32[896,896]{0,1:T(8,128)}) %all-reduce.6.cloned.1.call-update) | async-done | bytes 3211280 | tf_op jit(solution)/shard_map/psum | solution.py:12
  668.6 11.7 %cholesky.665 = f32[128,128]{1,0:T(8,128)S(1)} custom-call(f32[128,128]{1,0:T(8,128)S(1)} %cholesky.818), custom_call_target="Cholesky" | custom-call | tf_op jit(solution)/shard_map/jit(cholesky)/cholesky | solution.py:13
  681.0 9.8 custom-call.55
  697.2 11.7 %cholesky.684 = f32[128,128]{1,0:T(8,128)S(1)} custom-call(f32[128,128]{1,0:T(8,128)S(1)} %cholesky.822), custom_call_target="Cholesky" | custom-call | tf_op jit(solution)/shard_map/jit(cholesky)/cholesky | solution.py:13
  710.2 9.9 custom-call.56
  724.9 13.2 %cholesky.705 = f32[128,128]{1,0:T(8,128)} custom-call(f32[128,128]{1,0:T(8,128)} %cholesky.827), custom_call_target="Cholesky" | custom-call | tf_op jit(solution)/shard_map/jit(cholesky)/cholesky | solution.py:13
  740.2 11.3 %custom-call.57 = f32[1,128,128]{1,2,0:T(8,128)} custom-call(f32[1,128,128]{2,1,0:T(8,128)} %get-tuple-element.88), custom_call_target="InvertDiagBlocksLowerTriangular" | custom-call | tf_op jit(solution)/shard_map/jit(cholesky)/cholesky | solution.py:13
  755.5 12.5 %cholesky.724 = f32[128,128]{1,0:T(8,128)} custom-call(f32[128,128]{1,0:T(8,128)S(1)} %cholesky.832), custom_call_target="Cholesky" | custom-call | tf_op jit(solution)/shard_map/jit(cholesky)/cholesky | solution.py:13
  770.1 10.4 %custom-call.58 = f32[1,128,128]{1,2,0:T(8,128)} custom-call(f32[1,128,128]{2,1,0:T(8,128)S(1)} %get-tuple-element.85), custom_call_target="InvertDiagBlocksLowerTriangular" | custom-call | tf_op jit(solution)/shard_map/jit(cholesky)/cholesky | solution.py:13
  784.4 11.7 %cholesky.743 = f32[128,128]{1,0:T(8,128)S(1)} custom-call(f32[128,128]{1,0:T(8,128)S(1)} %cholesky.837), custom_call_target="Cholesky" | custom-call | tf_op jit(solution)/shard_map/jit(cholesky)/cholesky | solution.py:13
  810.1 12.2 %cholesky.762 = f32[128,128]{1,0:T(8,128)S(1)} custom-call(f32[128,128]{1,0:T(8,128)S(1)} %cholesky.842), custom_call_target="Cholesky" | custom-call | tf_op jit(solution)/shard_map/jit(cholesky)/cholesky | solution.py:13
  835.9 11.7 %cholesky.779 = f32[128,128]{1,0:T(8,128)S(1)} custom-call(f32[128,128]{1,0:T(8,128)S(1)} %convolution_subtract_fusion.18), custom_call_target="Cholesky" | custom-call | tf_op jit(solution)/shard_map/jit(cholesky)/cholesky | solution.py:13
  853.2 15.9 %fusion.6 = f32[896,896]{1,0:T(8,128)} fusion(f32[896,896]{1,0:T(8,128)} %get-tuple-element.77, f32[896,896]{1,0:T(8,128)S(1)} %get-tuple-element.96, pred[]{:T(512)S(6)} %cholesky.784, pred[]{:T(512)S(6)} %cholesky.655), kind=kOutput, calls=%fused_computation.13 | convolution fusion | flops 8636694528 | bytes 9633794 | tf_op jit(solution)/shard_map/dot_general | solution.py:24
  873.0 21.1 %while.5 = (s32[]{:T(128)}, f32[896,896]{1,0:T(8,128)}, s32[7,2]{0,1:T(2,128)S(1)}, f32[7,128,128]{2,1,0:T(8,128)S(1)}, s32[]{:T(128)}) while((s32[]{:T(128)}, f32[896,896]{1,0:T(8,128)}, s32[7,2]{0,1:T(2,128)S(1)}, f32[7,128,128]{2,1,0:T(8,128)S(1)}, s32[]{:T(128)}) %tuple.111), condition=%wide.while_cond.clone, body=%wide.while_body.clone.sunk | while | flops 2 | bytes 131189 | solution.py:14
  894.1 69.0 %custom-call.61 = f32[7,128,128]{1,2,0:T(8,128)S(1)} custom-call(f32[7,128,128]{2,1,0:T(8,128)S(1)} %get-tuple-element.19), custom_call_target="InvertDiagBlocksLowerTriangular" | custom-call | tf_op jit(solution)/shard_map/triangular_solve/custom-call.6 | solution.py:14
  (187 shorter events, 220.0 us)
Async XLA Ops:
  7.2 172.1 %all-reduce.4.cloned.1.call-start = ((), (), s32[]{:S(2)}) async-start(), calls=%async_computation | async-start | bytes 6422528 | tf_op jit(solution)/shard_map/psum | solution.py:12
  22.9 636.1 %all-reduce.6.cloned.1.call-start = ((), (), s32[]{:S(2)}) async-start(), calls=%async_computation.1 | async-start | bytes 6422528 | tf_op jit(solution)/shard_map/psum | solution.py:12
  179.3 4.6 copy-start.2
  186.2 1.7 copy-start.6
  212.6 0.7 copy-start.15
  459.7 4.2 copy-start.17
  459.7 5.0 copy-start.9
  461.7 11.2 %copy-start = (f32[128,1024]{1,0:T(8,128)}, f32[128,1024]{1,0:T(8,128)S(1)}, u32[]{:S(2)}) copy-start(f32[128,1024]{1,0:T(8,128)S(1)} %get-tuple-element.116) | copy-start | bytes 1572868
  464.6 8.3 copy-start.3
  468.3 9.3 copy-start.7
  472.9 6.4 copy-start.12
  666.9 1.7 copy-start.5
  696.4 0.7 copy-start.14
  869.1 94.0 %copy-start.1 = (f32[128,1024]{1,0:T(8,128)S(1)}, f32[128,1024]{1,0:T(8,128)}, u32[]{:S(2)}) copy-start(f32[128,1024]{1,0:T(8,128)} %copy-done) | copy-start | bytes 1572868
  873.0 91.7 %copy-start.4 = (f32[1024,128]{0,1:T(8,128)S(1)}, f32[1024,128]{0,1:T(8,128)}, u32[]{:S(2)}) copy-start(f32[1024,128]{0,1:T(8,128)} %copy-done.3) | copy-start | bytes 1572868
  963.1 4.5 copy-start.8
  966.1 4.6 copy-start.13
  970.7 3.7 copy-start.16
  974.4 3.8 copy-start.11
  978.1 4.2 copy-start.10
Sparse Core Ops, SparseCore 0:
  23.0 156.2 all-reduce.3
  507.5 151.3 all-reduce.5
where the time goes:
time: 1010 us; the launch traced here: 999 us
  other arithmetic  459 us (45%)
  waiting for transfers between devices  308 us (30%)
  matrix products  138 us (14%)
  local copies, waits for them, and re-layouts  69.3 us (7%)
  between operations  23.7 us (2%)
    another operation x53, other arithmetic, sweep_local(): low_fac = jnp.linalg.cholesky(gram_mat)  308 us
    psum x2, waiting for transfers between devices, sweep_local(): gram_mat = lax.psum(part_gram, GROUP_AXES)  308 us
    another operation x5, other arithmetic, sweep_local(): lax.linalg.triangular_solve(low_fac, row_blk, left_side=False, lower=True...  145 us
    another operation x26, matrix products, sweep_local(): lax.linalg.triangular_solve(low_fac, row_blk, left_side=False, lower=True...  57.2 us
    another operation x45, local copies, waits for them, and re-layouts, sweep_local(): lax.linalg.triangular_solve(low_fac, row_blk, left_side=False, lower=True...  46.6 us
    another operation x24, matrix products, sweep_local(): low_fac = jnp.linalg.cholesky(gram_mat)  36 us
    dot_general x2, matrix products, sweep_local(): lax.dot_general(row_blk, row_blk, (((0,), (0,)), ((), ())), precision=FUL...  29.3 us
  transfers between devices with their start and end apart: 2, of which 2 were waited for; matrix products, arithmetic and copies ran while one was open for 0% of the time, Pallas kernels for 0%

commit v1 on v0

v1 whole, which is shorter than its diff:
```python
import functools
import jax, jax.numpy as jnp
from jax import lax
from jax.experimental import pallas as pl
from jax.experimental.pallas import tpu as pltpu

HI = lax.Precision.HIGHEST
N = 896
B = 128
NB = N // B


def dot(a, b, ca, cb):
    return lax.dot_general(a, b, (((ca,), (cb,)), ((), ())), precision=HI, preferred_element_type=jnp.float32)


def factor_diag(diag):
    ng = B // 8
    sub = lax.broadcasted_iota(jnp.int32, (8, B), 0)
    lane = lax.broadcasted_iota(jnp.int32, (8, B), 1)
    rows = list(diag)
    inv = [jnp.where(lane == sub + 8 * q, 1.0, 0.0).astype(jnp.float32) for q in range(ng)]
    for p in range(ng):
        cols = [jnp.broadcast_to(rows[p][:, 8 * p + k:8 * p + k + 1], (8, B)) for k in range(8)]
        u = [None] * 8
        ux = [None] * 8
        rec = [None] * 8
        cross = {}
        scale = jnp.zeros((8, B), jnp.float32)
        dp, xp = rows[p], inv[p]
        for k in range(8):
            piv = jnp.broadcast_to(cols[k][k:k + 1, :], (8, B))
            rec[k] = 1.0 / piv
            scale = jnp.where(sub == k, piv, scale)
            low = jnp.where(sub > k, cols[k] * rec[k], 0.0)
            u[k] = jnp.broadcast_to(dp[k:k + 1, :], (8, B))
            ux[k] = jnp.broadcast_to(xp[k:k + 1, :], (8, B))
            for kk in range(k + 1, 8):
                cross[k, kk] = jnp.broadcast_to(cols[kk][k:k + 1, :], (8, B))
                cols[kk] = cols[kk] - low * cross[k, kk]
            dp = dp - low * u[k]
            xp = xp - low * ux[k]
        rs = lax.rsqrt(scale)
        rows[p] = dp * rs
        inv[p] = xp * rs
        for q in range(p + 1, ng):
            cq = [jnp.broadcast_to(rows[q][:, 8 * p + k:8 * p + k + 1], (8, B)) for k in range(8)]
            dq, xq = rows[q], inv[q]
            for k in range(8):
                low = cq[k] * rec[k]
                for kk in range(k + 1, 8):
                    cq[kk] = cq[kk] - low * cross[k, kk]
                dq = dq - low * u[k]
                xq = xq - low * ux[k]
            rows[q], inv[q] = dq, xq
    for q in range(ng):
        rows[q] = jnp.where(lane >= sub + 8 * q, rows[q], 0.0)
    return rows, inv


def chol_kernel(g_ref, r_ref, x_ref, w, xd):
    ng = B // 8
    w[:, :N] = g_ref[...]
    w[:, N:] = jnp.zeros((N, N), jnp.float32)

    def step(j, _):
        r0 = pl.multiple_of(j * B, B)
        rr = pl.ds(r0, B)
        diag = [w[pl.ds(pl.multiple_of(r0 + 8 * q, 8), 8), pl.ds(r0, B)] for q in range(ng)]
        rows, inv = factor_diag(diag)
        for q in range(ng):
            w[pl.ds(pl.multiple_of(r0 + 8 * q, 8), 8), pl.ds(r0, B)] = rows[q]
            w[pl.ds(pl.multiple_of(r0 + 8 * q, 8), 8), pl.ds(pl.multiple_of(r0 + N, B), B)] = inv[q]
            xd[pl.ds(8 * q, 8), :] = inv[q]
        mid = pl.ds(pl.multiple_of(r0 + B, B), N - B)
        w[rr, mid] = dot(xd[...], w[rr, mid], 1, 0)
        win = pl.ds(pl.multiple_of(r0 + B, B), N)

        def trail(i, _):
            ri = pl.ds(pl.multiple_of(i * B, B), B)
            left = w[rr, ri]
            w[ri, win] = w[ri, win] - dot(left, w[rr, win], 0, 0)
            return 0

        lax.fori_loop(j + 1, NB, trail, 0)
        return 0

    lax.fori_loop(0, NB, step, 0)
    for i in range(NB):
        ri = pl.ds(i * B, B)
        if i:
            r_ref[ri, :i * B] = jnp.zeros((B, i * B), jnp.float32)
        r_ref[ri, i * B:] = w[ri, i * B:N]
        x_ref[ri, :(i + 1) * B] = w[ri, N:N + (i + 1) * B]
        if i < NB - 1:
            x_ref[ri, (i + 1) * B:] = jnp.zeros((B, N - (i + 1) * B), jnp.float32)


def chol_inv(g):
    return pl.pallas_call(
        chol_kernel,
        out_shape=[jax.ShapeDtypeStruct((N, N), jnp.float32)] * 2,
        in_specs=[pl.BlockSpec(memory_space=pltpu.VMEM)],
        out_specs=[pl.BlockSpec(memory_space=pltpu.VMEM)] * 2,
        scratch_shapes=[pltpu.VMEM((N, 2 * N), jnp.float32), pltpu.VMEM((B, B), jnp.float32)],
        compiler_params=pltpu.CompilerParams(vmem_limit_bytes=56 * 2**20),
        name="chol_inv",
    )(g)


GROUP_AXES = ("outer", "rows")


def solution(mesh):
    from jax.sharding import PartitionSpec as P
    row_spec = P(("batch", "outer", "rows"), None)

    def local_qr(a):
        g1 = lax.psum(dot(a, a, 0, 0), GROUP_AXES)
        r1, x1 = chol_inv(g1)
        q1 = dot(a, x1, 1, 1)
        g2 = lax.psum(dot(q1, q1, 0, 0), GROUP_AXES)
        r2, x2 = chol_inv(g2)
        return dot(q1, x2, 1, 1), dot(r2, r1, 1, 0)

    return jax.shard_map(local_qr, mesh=mesh, in_specs=(row_spec,), out_specs=(row_spec, P("batch", None)), check_vma=False)
```

time: 1010 us -> 517 us (0.51)
  other arithmetic: 459 us -> 0 us
  Pallas kernels: 0 us -> 99.7 us
  local copies, waits for them, and re-layouts: 69.3 us -> 1.79 us
  matrix products: 138 us -> 84.9 us
    another operation x58 -> x0, other arithmetic: 454 us -> none  [the longest x53 308 us: sweep_local(): low_fac = jnp.linalg.cholesky(gram_mat)]
    pallas_call x0 -> x2, Pallas kernels: none -> 99.7 us  [chol_inv(): pl.pallas_call(chol_kernel, out_shape=[jax.ShapeDtypeStruct((N, N), jnp.f...]
    another operation x50 -> x0, matrix products: 93.2 us -> none  [the longest x26 57.2 us: sweep_local(): lax.linalg.triangular_solve(low_fac, row_blk, left_side=False, lower=True...]
    another operation x59 -> x0, local copies, waits for them, and re-layouts: 50 us -> none  [the longest x45 46.6 us: sweep_local(): lax.linalg.triangular_solve(low_fac, row_blk, left_side=False, lower=True...]
    dot_general x3 -> x5, matrix products: 45.2 us -> 84.9 us  [dot(): lax.dot_general(a, b, (((ca,), (cb,)), ((), ())), precision=HI, preferred...]
where the time goes in v1:
time: 517 us; the launch traced here: 509 us
  waiting for transfers between devices  308 us (60%)
  Pallas kernels  99.7 us (19%)
  matrix products  84.9 us (16%)
  between operations  14.5 us (3%)
    psum x1, waiting for transfers between devices, local_qr(): g1 = lax.psum(dot(a, a, 0, 0), GROUP_AXES)  156 us
    psum x1, waiting for transfers between devices, local_qr(): g2 = lax.psum(dot(q1, q1, 0, 0), GROUP_AXES)  152 us
    pallas_call x2, Pallas kernels, chol_inv(): pl.pallas_call(chol_kernel, out_shape=[jax.ShapeDtypeStruct((N, N), jnp.f...  99.7 us
    dot_general x5, matrix products, dot(): lax.dot_general(a, b, (((ca,), (cb,)), ((), ())), precision=HI, preferred...  84.9 us
  transfers between devices with their start and end apart: 2, of which 2 were waited for; matrix products, arithmetic and copies ran while one was open for 0% of the time, Pallas kernels for 0%

profile of v1, /device:TPU:1, one launch (start us, length us, event | category | flops | bytes accessed | tf_op | source)
XLA Modules:
  0.0 509.0 jit_solution(9987693745216183729)
XLA Ops:
  7.2 0.0 all-reduce.3.cloned.1.call-start
  7.2 15.6 %fusion = f32[896,896]{1,0:T(8,128)} fusion(f32[1024,896]{1,0:T(8,128)} %param.1), kind=kOutput, calls=%fused_computation | convolution fusion | flops 9865003008 | bytes 6881280 | tf_op jit(solution)/shard_map/dot_general | solution.py:14
  22.8 0.0 all-reduce.3.cloned.1.call-update
  22.8 0.0 all-reduce.5.cloned.1.call-start
  22.9 156.4 %all-reduce.3.cloned.1.call-done.g_ref = f32[896,896]{1,0:T(8,128)} async-done(((f32[896,896]{1,0:T(8,128)}), f32[896,896]{1,0:T(8,128)}) %all-reduce.3.cloned.1.call-update) | async-done | bytes 3211280 | tf_op jit(solution)/shard_map/psum | solution.py:119
  179.3 50.0 %chol_inv.2 = (f32[896,896]{1,0:T(8,128)}, f32[896,896]{1,0:T(8,128)}) custom-call(f32[896,896]{1,0:T(8,128)} %all-reduce.3.cloned.1.call-done.g_ref), custom_call_target="tpu_custom_call" | custom-call | tf_op jit(solution)/shard_map/chol_inv/pallas_call | solution.py:100
  229.3 15.2 %fusion.1 = f32[896,1024]{1,0:T(8,128)S(1)} fusion(f32[896,896]{1,0:T(8,128)} %get-tuple-element.6, f32[1024,896]{1,0:T(8,128)} %param.1), kind=kOutput, calls=%fused_computation.1 | convolution fusion | flops 9865003008 | bytes 10551296 | tf_op jit(solution)/shard_map/dot_general | solution.py:14
  244.5 0.0 copy-start.2
  244.5 1.8 copy-done.2
  246.3 13.7 %fusion.2 = f32[896,896]{1,0:T(8,128)} fusion(f32[896,1024]{1,0:T(8,128)S(1)} %fusion.1), kind=kOutput, calls=%fused_computation.2 | convolution fusion | flops 9865003008 | bytes 6881280 | tf_op jit(solution)/shard_map/dot_general | solution.py:14
  259.9 0.0 all-reduce.5.cloned.1.call-update
  260.0 151.6 %all-reduce.5.cloned.1.call-done.g_ref = f32[896,896]{1,0:T(8,128)} async-done(((f32[896,896]{1,0:T(8,128)}), f32[896,896]{1,0:T(8,128)}) %all-reduce.5.cloned.1.call-update) | async-done | bytes 3211280 | tf_op jit(solution)/shard_map/psum | solution.py:122
  411.5 49.7 %chol_inv.3 = (f32[896,896]{1,0:T(8,128)}, f32[896,896]{1,0:T(8,128)}) custom-call(f32[896,896]{1,0:T(8,128)} %all-reduce.5.cloned.1.call-done.g_ref), custom_call_target="tpu_custom_call" | custom-call | tf_op jit(solution)/shard_map/chol_inv/pallas_call | solution.py:100
  461.3 0.0 copy-start
  461.3 0.0 copy-start.1
  461.3 27.3 %fusion.3 = f32[1024,896]{1,0:T(8,128)} fusion(f32[896,1024]{1,0:T(8,128)} %copy-done.2, f32[896,896]{1,0:T(8,128)} %get-tuple-element.7), kind=kOutput, calls=%fused_computation.3 | convolution fusion | flops 9865003008 | bytes 10551296 | tf_op jit(solution)/shard_map/dot_general | solution.py:14
  488.5 0.0 copy-done
  488.5 0.0 copy-done.1
  488.6 13.2 %fusion.4 = f32[896,896]{1,0:T(8,128)} fusion(f32[896,896]{1,0:T(8,128)S(1)} %copy-done.1, f32[896,896]{1,0:T(8,128)S(1)} %copy-done), kind=kOutput, calls=%fused_computation.4 | convolution fusion | flops 8631877632 | bytes 9633792 | tf_op jit(solution)/shard_map/dot_general | solution.py:14
Async XLA Ops:
  7.2 172.1 %all-reduce.3.cloned.1.call-start = ((), (), s32[]{:S(2)}) async-start(), calls=%async_computation | async-start | bytes 6422528 | tf_op jit(solution)/shard_map/psum | solution.py:119
  22.8 388.7 %all-reduce.5.cloned.1.call-start = ((), (), s32[]{:S(2)}) async-start(), calls=%async_computation.1 | async-start | bytes 6422528 | tf_op jit(solution)/shard_map/psum | solution.py:122
  244.5 1.8 copy-start.2
  461.3 27.3 %copy-start = (f32[896,896]{1,0:T(8,128)S(1)}, f32[896,896]{1,0:T(8,128)}, u32[]{:S(2)}) copy-start(f32[896,896]{1,0:T(8,128)} %get-tuple-element.9) | copy-start | bytes 9633796
  461.3 27.3 %copy-start.1 = (f32[896,896]{1,0:T(8,128)S(1)}, f32[896,896]{1,0:T(8,128)}, u32[]{:S(2)}) copy-start(f32[896,896]{1,0:T(8,128)} %get-tuple-element.8) | copy-start | bytes 9633796
Sparse Core Ops, SparseCore 0:
  22.9 156.2 all-reduce.2
  260.1 151.4 all-reduce.4

commit v2 on v1

--- a/solution.py
+++ b/solution.py
@@ -1,8 +1,8 @@
-import functools
 import jax, jax.numpy as jnp
 from jax import lax
 from jax.experimental import pallas as pl
 from jax.experimental.pallas import tpu as pltpu
+from jax.sharding import PartitionSpec as P
 
 HI = lax.Precision.HIGHEST
 N = 896
@@ -60,8 +60,10 @@
 
 def chol_kernel(g_ref, r_ref, x_ref, w, xd):
     ng = B // 8
-    w[:, :N] = g_ref[...]
-    w[:, N:] = jnp.zeros((N, N), jnp.float32)
+    w[...] = jnp.zeros((N, 2 * N), jnp.float32)
+    for i in range(NB):
+        for j in range(i, NB):
+            w[i * B:(i + 1) * B, j * B:(j + 1) * B] = g_ref[pl.ds(block_row(i, j), B), :]
 
     def step(j, _):
         r0 = pl.multiple_of(j * B, B)
@@ -108,19 +110,210 @@
     )(g)
 
 
-GROUP_AXES = ("outer", "rows")
+CH = 32
+PIECE = 8 * CH
+HALF = 8 * PIECE
+ROWS_PACKED = 2 * HALF
+MESH_T = pl.DeviceIdType.MESH
+ORDER = (7, 3, 5, 6, 1, 2, 4)
+
+
+def _bits(d):
+    return tuple((d >> s) & 1 for s in range(3))
+
+
+def _flip(v, kind):
+    return (1 - kind) * (v + 1 - 2 * (v % 2)) + kind * (3 - v)
+
+
+def _label(v, kind):
+    return (1 - kind) * ((v % 2 + v // 2) % 2) + kind * (v // 2)
+
+
+def ar_kernel(p_ref, o_ref, rec0, acc0, rec1, acc1, rec2, s0, t0, s1, t1, s2, t2, s3, t3, s4, t4, s5, t5):
+    outer, row = lax.axis_index("outer"), lax.axis_index("rows")
+    pos = (row // 2, outer % 4, outer // 4)
+    core = row % 2
+    kinds = (core, 1 - core)
+    labels = [tuple(_label(v, k) for v in pos) for k in kinds]
+
+    def peer(stage, d):
+        x, y, z = (_flip(v, kinds[stage]) if b else v for v, b in zip(pos, _bits(d)))
+        return {"outer": z * 4 + y, "rows": x * 2 + core}
+
+    def index(stage, d):
+        return sum((1 - v if b else v) * (1 << s) for s, (v, b) in enumerate(zip(labels[stage], _bits(d))))
+
+    partner = {"outer": outer, "rows": pos[0] * 2 + 1 - core}
+    everyone = [partner] + [peer(s, d) for s in range(2) for d in range(1, 8)]
+
+    barrier = pltpu.get_barrier_semaphore()
+    for dev in everyone:
+        pl.semaphore_signal(barrier, inc=1, device_id=dev, device_id_type=MESH_T)
+    pl.semaphore_wait(barrier, len(everyone))
+
+    def copy(src, dst, send, recv, dev):
+        return pltpu.make_async_remote_copy(src_ref=src, dst_ref=dst, send_sem=send, recv_sem=recv, device_id=dev, device_id_type=MESH_T)
+
+    def piece(half, i):
+        return pl.ds(pl.multiple_of(half * HALF + i * PIECE, PIECE), PIECE)
+
+    sent = []
+
+    def go(c):
+        c.start()
+        sent.append(c)
+        return c
+
+    first = [go(copy(p_ref.at[piece(1 - core, index(1, d))], rec0.at[d], s0.at[d], t0.at[d], partner)) for d in ORDER + (0,)]
+    out1 = {}
+    for n, d in enumerate(ORDER + (0,)):
+        first[n].wait_recv()
+        acc0[d] = p_ref[piece(core, index(0, d)), :] + rec0[d]
+        if d:
+            out1[d] = go(copy(acc0.at[d], rec1.at[d - 1], s1.at[d - 1], t1.at[d - 1], peer(0, d)))
+    for d in range(1, 8):
+        out1[d].wait_recv()
+    total = acc0[0]
+    for d in range(1, 8):
+        total = total + rec1[d - 1]
+    acc1[...] = total
+    out2 = {}
+    for e in ORDER:
+        rows = pl.ds(pl.multiple_of(index(1, e) * CH, CH), CH)
+        out2[e] = go(copy(acc1.at[rows], rec2.at[e - 1], s2.at[e - 1], t2.at[e - 1], peer(1, e)))
+    for e in range(1, 8):
+        out2[e].wait_recv()
+    total = acc1[pl.ds(pl.multiple_of(index(1, 0) * CH, CH), CH), :]
+    for e in range(1, 8):
+        total = total + rec2[e - 1]
+
+    def chunk(e):
+        return pl.ds(pl.multiple_of(core * HALF + index(0, 0) * PIECE + index(1, e) * CH, CH), CH)
+
+    o_ref[chunk(0), :] = total
+    for e in ORDER:
+        go(copy(o_ref.at[chunk(0)], o_ref.at[chunk(0)], s3.at[e - 1], t3.at[e - 1], peer(1, e)))
+    for e in range(1, 8):
+        copy(o_ref.at[chunk(e)], o_ref.at[chunk(e)], s3.at[e - 1], t3.at[e - 1], peer(1, e)).wait_recv()
+    mine = piece(core, index(0, 0))
+    for d in ORDER:
+        go(copy(o_ref.at[mine], o_ref.at[mine], s4.at[d - 1], t4.at[d - 1], peer(0, d)))
+    go(copy(o_ref.at[mine], o_ref.at[mine], s5.at[0], t5.at[0], partner))
+    for d in (1, 2, 4, 3, 5, 6, 7):
+        got = piece(core, index(0, d))
+        copy(o_ref.at[got], o_ref.at[got], s4.at[d - 1], t4.at[d - 1], peer(0, d)).wait_recv()
+        go(copy(o_ref.at[got], o_ref.at[got], s5.at[d], t5.at[d], partner))
+    for d in range(8):
+        got = piece(1 - core, index(1, d))
+        copy(o_ref.at[got], o_ref.at[got], s5.at[d], t5.at[d], partner).wait_recv()
+    for c in sent:
+        c.wait_send()
+
+
+def all_reduce(p, ident):
+    sems = []
+    for n in (8, 7, 7, 7, 7, 8):
+        sems += [pltpu.SemaphoreType.DMA((n,))] * 2
+    return pl.pallas_call(
+        ar_kernel,
+        out_shape=jax.ShapeDtypeStruct((ROWS_PACKED, B), jnp.float32),
+        in_specs=[pl.BlockSpec(memory_space=pltpu.VMEM)],
+        out_specs=pl.BlockSpec(memory_space=pltpu.VMEM),
+        scratch_shapes=[
+            pltpu.VMEM((8, PIECE, B), jnp.float32),
+            pltpu.VMEM((8, PIECE, B), jnp.float32),
+            pltpu.VMEM((7, PIECE, B), jnp.float32),
+            pltpu.VMEM((PIECE, B), jnp.float32),
+            pltpu.VMEM((7, CH, B), jnp.float32),
+        ] + sems,
+        compiler_params=pltpu.CompilerParams(collective_id=ident, has_side_effects=True),
+        name="sum_group",
+    )(p)
+
+
+M_LOC = 1024
+STEP = 256
+TILES = [(lo, min(lo + 256, N)) for lo in range(0, N, 256)]
+
+
+def block_row(i, j):
+    return (i * NB - i * (i - 1) // 2 + j - i) * B
+
+
+def add_gram(rows, p_ref):
+    for lo, hi in TILES:
+        c = dot(rows[:, :hi], rows[:, lo:hi], 0, 0)
+        for j in range(lo // B, hi // B):
+            for i in range(j + 1):
+                at = pl.ds(block_row(i, j), B)
+                p_ref[at, :] = p_ref[at, :] + c[i * B:(i + 1) * B, j * B - lo:(j + 1) * B - lo]
+
+
+def gram_kernel(a_ref, p_ref):
+    p_ref[...] = jnp.zeros(p_ref.shape, jnp.float32)
+
+    def body(s, _):
+        add_gram(a_ref.at[pl.ds(pl.multiple_of(s * STEP, STEP), STEP)], p_ref)
+        return 0
+
+    lax.fori_loop(0, M_LOC // STEP, body, 0)
+
+
+def solve_gram_kernel(a_ref, x_ref, q_ref, p_ref):
+    p_ref[...] = jnp.zeros(p_ref.shape, jnp.float32)
+
+    def body(s, _):
+        at = pl.ds(pl.multiple_of(s * STEP, STEP), STEP)
+        for lo, hi in TILES:
+            q_ref[at, lo:hi] = dot(a_ref[at, :hi], x_ref[lo:hi, :hi], 1, 1)
+        add_gram(q_ref.at[at], p_ref)
+        return 0
+
+    lax.fori_loop(0, M_LOC // STEP, body, 0)
+
+
+def solve_kernel(a_ref, x_ref, r2_ref, r1_ref, q_ref, r_ref):
+    def body(s, _):
+        at = pl.ds(pl.multiple_of(s * STEP, STEP), STEP)
+        for lo, hi in TILES:
+            q_ref[at, lo:hi] = dot(a_ref[at, :hi], x_ref[lo:hi, :hi], 1, 1)
+        return 0
+
+    lax.fori_loop(0, M_LOC // STEP, body, 0)
+    for lo, hi in TILES:
+        if lo:
+            r_ref[lo:hi, :lo] = jnp.zeros((hi - lo, lo), jnp.float32)
+        r_ref[lo:hi, lo:] = dot(r2_ref[lo:hi, lo:], r1_ref[lo:, lo:], 1, 0)
+
+
+def vm(n):
+    return [pl.BlockSpec(memory_space=pltpu.VMEM)] * n
+
+
+PARAMS = pltpu.CompilerParams(vmem_limit_bytes=56 * 2**20)
+F32 = lambda *s: jax.ShapeDtypeStruct(s, jnp.float32)
+
+
+def gram(a):
+    return pl.pallas_call(gram_kernel, out_shape=F32(ROWS_PACKED, B), in_specs=vm(1), out_specs=vm(1)[0], compiler_params=PARAMS, name="gram")(a)
+
+
+def solve_gram(a, x):
+    return pl.pallas_call(solve_gram_kernel, out_shape=[F32(M_LOC, N), F32(ROWS_PACKED, B)], in_specs=vm(2), out_specs=vm(2), compiler_params=PARAMS, name="solve_gram")(a, x)
+
+
+def solve(a, x, r2, r1):
+    return pl.pallas_call(solve_kernel, out_shape=[F32(M_LOC, N), F32(N, N)], in_specs=vm(4), out_specs=vm(2), compiler_params=PARAMS, name="solve")(a, x, r2, r1)
 
 
 def solution(mesh):
-    from jax.sharding import PartitionSpec as P
     row_spec = P(("batch", "outer", "rows"), None)
 
     def local_qr(a):
-        g1 = lax.psum(dot(a, a, 0, 0), GROUP_AXES)
-        r1, x1 = chol_inv(g1)
-        q1 = dot(a, x1, 1, 1)
-        g2 = lax.psum(dot(q1, q1, 0, 0), GROUP_AXES)
-        r2, x2 = chol_inv(g2)
-        return dot(q1, x2, 1, 1), dot(r2, r1, 1, 0)
+        r1, x1 = chol_inv(all_reduce(gram(a), 0))
+        q1, p2 = solve_gram(a, x1)
+        r2, x2 = chol_inv(all_reduce(p2, 1))
+        return tuple(solve(q1, x2, r2, r1))
 
     return jax.shard_map(local_qr, mesh=mesh, in_specs=(row_spec,), out_specs=(row_spec, P("batch", None)), check_vma=False)

time: 517 us -> 239 us (0.46); the launches traced: 509 us -> 237 us
  waiting for transfers between devices: 308 us -> 0 us
  Pallas kernels: 99.7 us -> 236 us
  matrix products: 84.9 us -> 0 us
  between operations: 14.5 us -> 0.65 us
    psum x2 -> x0, waiting for transfers between devices: 308 us -> none  [the longest x1 156 us: local_qr(): g1 = lax.psum(dot(a, a, 0, 0), GROUP_AXES)]
    pallas_call x0 -> x5, Pallas kernels: none -> 137 us  [the longest x2 81.5 us: all_reduce(): pl.pallas_call(ar_kernel, out_shape=jax.ShapeDtypeStruct((ROWS_PACKED, B)...]
    dot_general x5 -> x0, matrix products: 84.9 us -> none  [dot(): lax.dot_general(a, b, (((ca,), (cb,)), ((), ())), precision=HI, preferred...]
  transfers between devices with their start and end apart: 2 -> 0, of which waited for: 2 -> 0; matrix products, arithmetic and copies ran while one was open for 0% -> 0% of each run, Pallas kernels for 0% -> 0%
where the time goes in v2:
time: 239 us; the launch traced here: 237 us
  Pallas kernels  236 us (99%)
    pallas_call x2, Pallas kernels, chol_inv(): pl.pallas_call(chol_kernel, out_shape=[jax.ShapeDtypeStruct((N, N), jnp.f...  98.9 us
    pallas_call x2, Pallas kernels, all_reduce(): pl.pallas_call(ar_kernel, out_shape=jax.ShapeDtypeStruct((ROWS_PACKED, B)...  81.5 us
    pallas_call x1, Pallas kernels, solve_gram(): pl.pallas_call(solve_gram_kernel, out_shape=[F32(M_LOC, N), F32(ROWS_PACK...  21.8 us
    pallas_call x1, Pallas kernels, solve(): pl.pallas_call(solve_kernel, out_shape=[F32(M_LOC, N), F32(N, N)], in_spe...  21.4 us
    pallas_call x1, Pallas kernels, gram(): pl.pallas_call(gram_kernel, out_shape=F32(ROWS_PACKED, B), in_specs=vm(1)...  12.6 us

profile of v2, /device:TPU:1, one launch (start us, length us, event | category | flops | bytes accessed | tf_op | source)
XLA Modules:
  0.0 236.9 jit_solution(10623871976750259567)
XLA Ops:
  0.6 12.6 %gram.1.p_ref = f32[4096,128]{1,0:T(8,128)} custom-call(f32[1024,896]{1,0:T(8,128)} %a_ref.3), custom_call_target="tpu_custom_call" | custom-call | tf_op jit(solution)/shard_map/gram/pallas_call | solution.py:299
  13.2 43.1 %sum_group.2.g_ref = f32[4096,128]{1,0:T(8,128)} custom-call(f32[4096,128]{1,0:T(8,128)} %gram.1.p_ref), custom_call_target="tpu_custom_call" | custom-call | tf_op jit(solution)/shard_map/sum_group/pallas_call | solution.py:218
  56.3 49.5 %chol_inv.2 = (f32[896,896]{1,0:T(8,128)}, f32[896,896]{1,0:T(8,128)}) custom-call(f32[4096,128]{1,0:T(8,128)} %sum_group.2.g_ref), custom_call_target="tpu_custom_call" | custom-call | tf_op jit(solution)/shard_map/chol_inv/pallas_call | solution.py:102
  105.8 21.8 %solve_gram.1 = (f32[1024,896]{1,0:T(8,128)}, f32[4096,128]{1,0:T(8,128)}) custom-call(f32[1024,896]{1,0:T(8,128)} %a_ref.3, f32[896,896]{1,0:T(8,128)} %get-tuple-element.8.x_ref), custom_call_target="tpu_custom_call" | custom-call | tf_op jit(solution)/shard_map/solve_gram/pallas_call | solution.py:303
  127.6 38.4 %sum_group.3.g_ref = f32[4096,128]{1,0:T(8,128)} custom-call(f32[4096,128]{1,0:T(8,128)} %get-tuple-element.10.p_ref), custom_call_target="tpu_custom_call" | custom-call | tf_op jit(solution)/shard_map/sum_group/pallas_call | solution.py:218
  166.0 49.5 %chol_inv.3 = (f32[896,896]{1,0:T(8,128)}, f32[896,896]{1,0:T(8,128)}) custom-call(f32[4096,128]{1,0:T(8,128)} %sum_group.3.g_ref), custom_call_target="tpu_custom_call" | custom-call | tf_op jit(solution)/shard_map/chol_inv/pallas_call | solution.py:102
  215.4 21.4 %solve.1 = (f32[1024,896]{1,0:T(8,128)}, f32[896,896]{1,0:T(8,128)}) custom-call(f32[1024,896]{1,0:T(8,128)} %get-tuple-element.9.a_ref, f32[896,896]{1,0:T(8,128)} %get-tuple-element.11.x_ref, f32[896,896]{1,0:T(8,128)} %get-tuple-element.12.r2_ref, f32[896,896]{1,0:T(8,128)} %get-tuple-element.13.r1_ref), custom_call_target="tpu_custom_call" | custom-call | tf_op jit(solution)/shard_map/solve/pallas_call | solution.py:307

commit v3 on v2

v3 whole, which is shorter than its diff:
```python
import jax
import jax.numpy as jnp
from jax import lax
from jax.experimental import pallas as pl
from jax.experimental.pallas import tpu as pltpu
from jax.sharding import PartitionSpec as P

HI = lax.Precision.HIGHEST
N = 896
B = 128
NB = N // B
NG = B // 8


def dot(a, b, ca, cb):
    return lax.dot_general(a, b, (((ca,), (cb,)), ((), ())), precision=HI, preferred_element_type=jnp.float32)


def lane_col(v, c):
    lane = lax.broadcasted_iota(jnp.int32, (8, B), 1)
    return jnp.broadcast_to(jnp.sum(jnp.where(lane == c, v, 0.0), axis=1, keepdims=True), (8, B))


def sub_row(v, k):
    return jnp.broadcast_to(v[k:k + 1, :], (8, B))


def factor_diag(diag):
    sub = lax.broadcasted_iota(jnp.int32, (8, B), 0)
    lane = lax.broadcasted_iota(jnp.int32, (8, B), 1)
    m = list(diag)
    rows, inv = [None] * NG, [None] * NG
    for p in range(NG):
        g0 = 8 * p
        here = (lane >= g0) & (lane < g0 + 8)
        cols = [lane_col(m[p], g0 + k) for k in range(8)]
        z = jnp.where(here, jnp.where(lane == sub + g0, 1.0, 0.0), m[p])
        near = p + 1 < NG
        if near:
            cq = [lane_col(m[p + 1], g0 + k) for k in range(8)]
            mq = jnp.where(here, 0.0, m[p + 1])
        recs = jnp.zeros((8, B), jnp.float32)
        pivs = jnp.ones((8, B), jnp.float32)
        for k in range(8):
            piv = sub_row(cols[k], k)
            rec = 1.0 / piv
            pivs = jnp.where(sub == k, piv, pivs)
            recs = jnp.where(sub == k, rec, recs)
            low = jnp.where(sub > k, cols[k] * rec, 0.0)
            for kk in range(k + 1, 8):
                cross = sub_row(cols[kk], k)
                cols[kk] = cols[kk] - low * cross
                if near:
                    if kk == k + 1:
                        lq = cq[k] * rec
                    cq[kk] = cq[kk] - lq * cross
            if near and k == 7:
                lq = cq[k] * rec
            uz = sub_row(z, k)
            z = z - low * uz
            if near:
                mq = mq - lq * uz
        scale = lax.rsqrt(pivs)
        upper = z
        for kk in range(8):
            upper = jnp.where(lane == g0 + kk, cols[kk], upper)
        rows[p] = jnp.where(lane >= sub + g0, upper * scale, 0.0)
        inv[p] = jnp.where(lane < g0 + 8, z * scale, 0.0)
        if p + 2 < NG:
            wv = z * recs
            for kk in range(7, 0, -1):
                wv = wv - jnp.where(sub < kk, cols[kk] * recs, 0.0) * sub_row(wv, kk)
            wk = [sub_row(wv, k) for k in range(8)]
            for q in range(p + 2, NG):
                new = jnp.where(here, 0.0, m[q])
                for k in range(8):
                    new = new - lane_col(m[q], g0 + k) * wk[k]
                m[q] = new
        if near:
            m[p + 1] = mq
    return rows, inv


def block_row(i, j):
    return (i * NB - i * (i - 1) // 2 + j - i) * B


def mult(x):
    return pl.multiple_of(x, B)


def factor(g_ref, w, xd):
    w[:, N:] = jnp.zeros((N, N), jnp.float32)
    for i in range(NB):
        for j in range(i):
            w[i * B:(i + 1) * B, j * B:(j + 1) * B] = jnp.zeros((B, B), jnp.float32)
        for j in range(i, NB):
            w[i * B:(i + 1) * B, j * B:(j + 1) * B] = g_ref[pl.ds(block_row(i, j), B), :]

    def step(j, _):
        r0 = mult(j * B)
        rr = pl.ds(r0, B)
        group = [pl.ds(pl.multiple_of(r0 + 8 * q, 8), 8) for q in range(NG)]
        rows, inv = factor_diag([w[gq, pl.ds(r0, B)] for gq in group])
        for q in range(NG):
            w[group[q], pl.ds(r0, B)] = rows[q]
            w[group[q], pl.ds(mult(r0 + N), B)] = inv[q]
            xd[pl.ds(8 * q, 8), :] = inv[q]
        mid = pl.ds(mult(r0 + B), N - B)
        w[rr, mid] = dot(xd[...], w[rr, mid], 1, 0)
        odd = j % 2

        def trail(top, depth):
            src = pl.ds(mult(top), depth)
            win = pl.ds(mult(top + depth), N)

            def body(i, _):
                ri = pl.ds(mult(i * B), B)
                w[ri, win] = w[ri, win] - dot(w[src, ri], w[src, win], 0, 0)
                return 0

            return body

        lax.fori_loop(j + 1, jnp.where(odd == 0, jnp.minimum(j + 2, NB), j + 1), trail(r0, B), 0)
        lax.fori_loop(jnp.where(odd == 1, j + 1, NB), NB, trail(jnp.maximum(r0 - B, 0), 2 * B), 0)
        return 0

    lax.fori_loop(0, NB, step, 0)
    for i in range(1, NB):
        w[i * B:(i + 1) * B, :i * B] = jnp.zeros((B, i * B), jnp.float32)


M_LOC = 1024
STEP = 256
NSTEP = M_LOC // STEP
TILES = [(lo, min(lo + 256, N)) for lo in range(0, N, 256)]


def add_gram(rows, p_ref):
    for lo, hi in TILES:
        c = dot(rows[:, :hi], rows[:, lo:hi], 0, 0)
        for j in range(lo // B, hi // B):
            for i in range(j + 1):
                at = pl.ds(block_row(i, j), B)
                p_ref[at, :] = p_ref[at, :] + c[i * B:(i + 1) * B, j * B - lo:(j + 1) * B - lo]


def solve_rows(a, w, q):
    for lo, hi in TILES:
        q[:, lo:hi] = dot(a[:, :hi], w[lo:hi, N:N + hi], 1, 1)


def rows_at(s):
    return pl.ds(pl.multiple_of(s * STEP, STEP), STEP)


def gram_kernel(a_hbm, p_ref, a, sem):
    loads = [pltpu.make_async_copy(a_hbm.at[rows_at(s)], a.at[rows_at(s)], sem.at[s]) for s in range(NSTEP)]
    for c in loads:
        c.start()
    p_ref[...] = jnp.zeros(p_ref.shape, jnp.float32)

    def body(s, _):
        pltpu.make_async_copy(a_hbm.at[rows_at(s)], a.at[rows_at(s)], sem.at[s]).wait()
        add_gram(a.at[rows_at(s)], p_ref)
        return 0

    lax.fori_loop(0, NSTEP, body, 0)


def sweep_one_kernel(g_ref, a_hbm, q_hbm, p_ref, r_hbm, w, xd, a, q, sem, qsem):
    load = pltpu.make_async_copy(a_hbm, a, sem.at[0])
    load.start()
    p_ref[...] = jnp.zeros(p_ref.shape, jnp.float32)
    factor(g_ref, w, xd)
    keep = pltpu.make_async_copy(w.at[:, pl.ds(0, N)], r_hbm, sem.at[1])
    keep.start()
    load.wait()

    def body(s, _):
        at = rows_at(s)
        solve_rows(a.at[at], w, q.at[at])
        pltpu.make_async_copy(q.at[at], q_hbm.at[at], qsem.at[s]).start()
        add_gram(q.at[at], p_ref)
        return 0

    lax.fori_loop(0, NSTEP, body, 0)
    for s in range(NSTEP):
        pltpu.make_async_copy(q.at[rows_at(s)], q_hbm.at[rows_at(s)], qsem.at[s]).wait()
    keep.wait()


def sweep_two_kernel(g_ref, a_hbm, r1_hbm, q_hbm, r_hbm, w, xd, a, q, r1, r, sem, qsem, rsem):
    load = pltpu.make_async_copy(a_hbm, a, sem.at[0])
    load.start()
    load_r = pltpu.make_async_copy(r1_hbm, r1, sem.at[1])
    load_r.start()
    factor(g_ref, w, xd)
    load.wait()

    def body(s, _):
        at = rows_at(s)
        solve_rows(a.at[at], w, q.at[at])
        pltpu.make_async_copy(q.at[at], q_hbm.at[at], qsem.at[s]).start()
        return 0

    lax.fori_loop(0, NSTEP, body, 0)
    load_r.wait()
    stores = []
    for n, (lo, hi) in enumerate(TILES):
        if lo:
            r[lo:hi, :lo] = jnp.zeros((hi - lo, lo), jnp.float32)
        for clo, chi in TILES[n:]:
            r[lo:hi, clo:chi] = dot(w[lo:hi, lo:chi], r1[lo:chi, clo:chi], 1, 0)
        at = pl.ds(lo, hi - lo)
        stores.append(pltpu.make_async_copy(r.at[at], r_hbm.at[at], rsem.at[n]))
        stores[-1].start()
    for s in range(NSTEP):
        pltpu.make_async_copy(q.at[rows_at(s)], q_hbm.at[rows_at(s)], qsem.at[s]).wait()
    for c in stores:
        c.wait()


VM = pl.BlockSpec(memory_space=pltpu.VMEM)
ANY = pl.BlockSpec(memory_space=pl.ANY)
PARAMS = pltpu.CompilerParams(vmem_limit_bytes=58 * 2**20)
DMA = pltpu.SemaphoreType.DMA


def out(*s):
    return jax.ShapeDtypeStruct(s, jnp.float32)


def buf(*s):
    return pltpu.VMEM(s, jnp.float32)


def gram(a):
    return pl.pallas_call(
        gram_kernel, out_shape=out(ROWS_PACKED, B), in_specs=[ANY], out_specs=VM, name="gram",
        scratch_shapes=[buf(M_LOC, N), DMA((NSTEP,))], compiler_params=PARAMS,
    )(a)


def sweep_one(g, a):
    return pl.pallas_call(
        sweep_one_kernel, out_shape=[out(M_LOC, N), out(ROWS_PACKED, B), out(N, N)], in_specs=[VM, ANY], out_specs=[ANY, VM, ANY],
        scratch_shapes=[buf(N, 2 * N), buf(B, B), buf(M_LOC, N), buf(M_LOC, N), DMA((2,)), DMA((NSTEP,))],
        compiler_params=PARAMS, name="sweep_one",
    )(g, a)


def sweep_two(g, q1, r1):
    return pl.pallas_call(
        sweep_two_kernel, out_shape=[out(M_LOC, N), out(N, N)], in_specs=[VM, ANY, ANY], out_specs=[ANY, ANY],
        scratch_shapes=[buf(N, 2 * N), buf(B, B), buf(M_LOC, N), buf(M_LOC, N), buf(N, N), buf(N, N), DMA((2,)), DMA((NSTEP,)), DMA((4,))],
        compiler_params=PARAMS, name="sweep_two",
    )(g, q1, r1)


CH = 32
PIECE = 8 * CH
HALF = 8 * PIECE
ROWS_PACKED = 2 * HALF
MESH_T = pl.DeviceIdType.MESH
ORDER = (7, 3, 5, 6, 1, 2, 4)


def _bits(d):
    return tuple((d >> s) & 1 for s in range(3))


def _flip(v, kind):
    return (1 - kind) * (v + 1 - 2 * (v % 2)) + kind * (3 - v)


def _label(v, kind):
    return (1 - kind) * ((v % 2 + v // 2) % 2) + kind * (v // 2)


def ar_kernel(p_ref, o_ref, rec0, acc0, rec1, acc1, rec2, s0, t0, s1, t1, s2, t2, s3, t3, s4, t4, s5, t5):
    outer, row = lax.axis_index("outer"), lax.axis_index("rows")
    pos = (row // 2, outer % 4, outer // 4)
    core = row % 2
    kinds = (core, 1 - core)
    labels = [tuple(_label(v, k) for v in pos) for k in kinds]

    def peer(stage, d):
        x, y, z = (_flip(v, kinds[stage]) if b else v for v, b in zip(pos, _bits(d)))
        return {"outer": z * 4 + y, "rows": x * 2 + core}

    def index(stage, d):
        return sum((1 - v if b else v) * (1 << s) for s, (v, b) in enumerate(zip(labels[stage], _bits(d))))

    partner = {"outer": outer, "rows": pos[0] * 2 + 1 - core}
    everyone = [partner] + [peer(s, d) for s in range(2) for d in range(1, 8)]

    barrier = pltpu.get_barrier_semaphore()
    for dev in everyone:
        pl.semaphore_signal(barrier, inc=1, device_id=dev, device_id_type=MESH_T)
    pl.semaphore_wait(barrier, len(everyone))

    def copy(src, dst, send, recv, dev):
        return pltpu.make_async_remote_copy(src_ref=src, dst_ref=dst, send_sem=send, recv_sem=recv, device_id=dev, device_id_type=MESH_T)

    def piece(half, i):
        return pl.ds(pl.multiple_of(half * HALF + i * PIECE, PIECE), PIECE)

    sent = []

    def go(c):
        c.start()
        sent.append(c)
        return c

    first = [go(copy(p_ref.at[piece(1 - core, index(1, d))], rec0.at[d], s0.at[d], t0.at[d], partner)) for d in ORDER + (0,)]
    out1 = {}
    for n, d in enumerate(ORDER + (0,)):
        first[n].wait_recv()
        acc0[d] = p_ref[piece(core, index(0, d)), :] + rec0[d]
        if d:
            out1[d] = go(copy(acc0.at[d], rec1.at[d - 1], s1.at[d - 1], t1.at[d - 1], peer(0, d)))
    for d in range(1, 8):
        out1[d].wait_recv()
    total = acc0[0]
    for d in range(1, 8):
        total = total + rec1[d - 1]
    acc1[...] = total
    out2 = {}
    for e in ORDER:
        rows = pl.ds(pl.multiple_of(index(1, e) * CH, CH), CH)
        out2[e] = go(copy(acc1.at[rows], rec2.at[e - 1], s2.at[e - 1], t2.at[e - 1], peer(1, e)))
    for e in range(1, 8):
        out2[e].wait_recv()
    total = acc1[pl.ds(pl.multiple_of(index(1, 0) * CH, CH), CH), :]
    for e in range(1, 8):
        total = total + rec2[e - 1]

    def chunk(e):
        return pl.ds(pl.multiple_of(core * HALF + index(0, 0) * PIECE + index(1, e) * CH, CH), CH)

    o_ref[chunk(0), :] = total
    for e in ORDER:
        go(copy(o_ref.at[chunk(0)], o_ref.at[chunk(0)], s3.at[e - 1], t3.at[e - 1], peer(1, e)))
    for e in range(1, 8):
        copy(o_ref.at[chunk(e)], o_ref.at[chunk(e)], s3.at[e - 1], t3.at[e - 1], peer(1, e)).wait_recv()
    mine = piece(core, index(0, 0))
    for d in ORDER:
        go(copy(o_ref.at[mine], o_ref.at[mine], s4.at[d - 1], t4.at[d - 1], peer(0, d)))
    go(copy(o_ref.at[mine], o_ref.at[mine], s5.at[0], t5.at[0], partner))
    for d in (1, 2, 4, 3, 5, 6, 7):
        got = piece(core, index(0, d))
        copy(o_ref.at[got], o_ref.at[got], s4.at[d - 1], t4.at[d - 1], peer(0, d)).wait_recv()
        go(copy(o_ref.at[got], o_ref.at[got], s5.at[d], t5.at[d], partner))
    for d in range(8):
        got = piece(1 - core, index(1, d))
        copy(o_ref.at[got], o_ref.at[got], s5.at[d], t5.at[d], partner).wait_recv()
    for c in sent:
        c.wait_send()


def all_reduce(p, ident):
    sems = []
    for n in (8, 7, 7, 7, 7, 8):
        sems += [pltpu.SemaphoreType.DMA((n,))] * 2
    return pl.pallas_call(
        ar_kernel,
        out_shape=jax.ShapeDtypeStruct((ROWS_PACKED, B), jnp.float32),
        in_specs=[pl.BlockSpec(memory_space=pltpu.VMEM)],
        out_specs=pl.BlockSpec(memory_space=pltpu.VMEM),
        scratch_shapes=[
            pltpu.VMEM((8, PIECE, B), jnp.float32),
            pltpu.VMEM((8, PIECE, B), jnp.float32),
            pltpu.VMEM((7, PIECE, B), jnp.float32),
            pltpu.VMEM((PIECE, B), jnp.float32),
            pltpu.VMEM((7, CH, B), jnp.float32),
        ] + sems,
        compiler_params=pltpu.CompilerParams(collective_id=ident, has_side_effects=True),
        name="sum_group",
    )(p)


def solution(mesh):
    row_spec = P(("batch", "outer", "rows"), None)

    def local_qr(a):
        q1, p2, r1 = sweep_one(all_reduce(gram(a), 0), a)
        return tuple(sweep_two(all_reduce(p2, 1), q1, r1))

    return jax.shard_map(local_qr, mesh=mesh, in_specs=(row_spec,), out_specs=(row_spec, P("batch", None)), check_vma=False)
```

time: 239 us -> 203 us (0.85)
  Pallas kernels: 236 us -> 200 us
    pallas_call x5 -> x3, Pallas kernels: 155 us -> 118 us  [the longest x1 55.7 us: sweep_one(): pl.pallas_call(sweep_one_kernel, out_shape=[out(M_LOC, N), out(ROWS_PACKE...]
where the time goes in v3:
time: 203 us; the launch traced here: 201 us
  Pallas kernels  200 us (99%)
    pallas_call x2, Pallas kernels, all_reduce(): pl.pallas_call(ar_kernel, out_shape=jax.ShapeDtypeStruct((ROWS_PACKED, B)...  81.6 us
    pallas_call x1, Pallas kernels, sweep_one(): pl.pallas_call(sweep_one_kernel, out_shape=[out(M_LOC, N), out(ROWS_PACKE...  55.7 us
    pallas_call x1, Pallas kernels, sweep_two(): pl.pallas_call(sweep_two_kernel, out_shape=[out(M_LOC, N), out(N, N)], in...  50.9 us
    pallas_call x1, Pallas kernels, gram(): pl.pallas_call(gram_kernel, out_shape=out(ROWS_PACKED, B), in_specs=[ANY]...  11.6 us

profile of v3, /device:TPU:1, one launch (start us, length us, event | category | flops | bytes accessed | tf_op | source)
XLA Modules:
  0.0 200.7 jit_solution(2180448406797431029)
XLA Ops:
  0.6 11.6 %gram.1.p_ref = f32[4096,128]{1,0:T(8,128)} custom-call(f32[1024,896]{1,0:T(8,128)} %a_hbm.3), custom_call_target="tpu_custom_call" | custom-call | tf_op jit(solution)/shard_map/gram/pallas_call | solution.py:239
  12.2 43.1 %sum_group.2.g_ref = f32[4096,128]{1,0:T(8,128)} custom-call(f32[4096,128]{1,0:T(8,128)} %gram.1.p_ref), custom_call_target="tpu_custom_call" | custom-call | tf_op jit(solution)/shard_map/sum_group/pallas_call | solution.py:366
  55.4 55.7 %sweep_one.1 = (f32[1024,896]{1,0:T(8,128)}, f32[4096,128]{1,0:T(8,128)}, f32[896,896]{1,0:T(8,128)}) custom-call(f32[4096,128]{1,0:T(8,128)} %sum_group.2.g_ref, f32[1024,896]{1,0:T(8,128)} %a_hbm.3), custom_call_target="tpu_custom_call" | custom-call | tf_op jit(solution)/shard_map/sweep_one/pallas_call | solution.py:246
  111.1 38.5 %sum_group.3.g_ref = f32[4096,128]{1,0:T(8,128)} custom-call(f32[4096,128]{1,0:T(8,128)} %get-tuple-element.5.p_ref), custom_call_target="tpu_custom_call" | custom-call | tf_op jit(solution)/shard_map/sum_group/pallas_call | solution.py:366
  149.6 50.9 %sweep_two.1 = (f32[1024,896]{1,0:T(8,128)}, f32[896,896]{1,0:T(8,128)}) custom-call(f32[4096,128]{1,0:T(8,128)} %sum_group.3.g_ref, f32[1024,896]{1,0:T(8,128)} %get-tuple-element.6.a_hbm, f32[896,896]{1,0:T(8,128)} %get-tuple-element.7.r1_hbm), custom_call_target="tpu_custom_call" | custom-call | tf_op jit(solution)/shard_map/sweep_two/pallas_call | solution.py:254

commit v4 on v3

--- a/solution.py
+++ b/solution.py
@@ -259,11 +259,11 @@
 
 
 CH = 32
-PIECE = 8 * CH
-HALF = 8 * PIECE
-ROWS_PACKED = 2 * HALF
+PAIR = 2 * CH
+ROWS_PACKED = 128 * CH
+SUMS = (2, 8, 4, PAIR, B)
 MESH_T = pl.DeviceIdType.MESH
-ORDER = (7, 3, 5, 6, 1, 2, 4)
+FAR_FIRST = (7, 3, 5, 6, 1, 2, 4)
 
 
 def _bits(d):
@@ -278,7 +278,7 @@
     return (1 - kind) * ((v % 2 + v // 2) % 2) + kind * (v // 2)
 
 
-def ar_kernel(p_ref, o_ref, rec0, acc0, rec1, acc1, rec2, s0, t0, s1, t1, s2, t2, s3, t3, s4, t4, s5, t5):
+def ar_kernel(p_hbm, o_hbm, p, o, rec0, acc0, rec1, acc1, rec2, ld, st, s0, t0, s1, t1, s2, t2, s3, t3, s4, t4, s5, t5):
     outer, row = lax.axis_index("outer"), lax.axis_index("rows")
     pos = (row // 2, outer % 4, outer // 4)
     core = row % 2
@@ -292,19 +292,31 @@
     def index(stage, d):
         return sum((1 - v if b else v) * (1 << s) for s, (v, b) in enumerate(zip(labels[stage], _bits(d))))
 
+    def group(stage, g):
+        return sum((1 - labels[stage][s] if (g >> (s - 1)) & 1 else labels[stage][s]) * (1 << (s - 1)) for s in (1, 2))
+
+    def inside(e):
+        v = labels[1][0]
+        return pl.ds(pl.multiple_of((1 - v if e & 1 else v) * CH, CH), CH)
+
     partner = {"outer": outer, "rows": pos[0] * 2 + 1 - core}
-    everyone = [partner] + [peer(s, d) for s in range(2) for d in range(1, 8)]
-
+    peers = [{d: peer(s, d) for d in range(1, 8)} for s in range(2)]
+    idx = [index(0, d) for d in range(8)]
+    grp = [[group(s, g) for g in range(4)] for s in range(2)]
+    last_first = (3, 2, 1, 0)
+
+    loads = [pltpu.make_async_copy(p_hbm.at[h], p.at[h], ld.at[n]) for n, h in enumerate((1 - core, core))]
+    for c in loads:
+        c.start()
     barrier = pltpu.get_barrier_semaphore()
+    everyone = [partner, *peers[0].values(), *peers[1].values()]
     for dev in everyone:
         pl.semaphore_signal(barrier, inc=1, device_id=dev, device_id_type=MESH_T)
+    loads[0].wait()
     pl.semaphore_wait(barrier, len(everyone))
 
     def copy(src, dst, send, recv, dev):
         return pltpu.make_async_remote_copy(src_ref=src, dst_ref=dst, send_sem=send, recv_sem=recv, device_id=dev, device_id_type=MESH_T)
-
-    def piece(half, i):
-        return pl.ds(pl.multiple_of(half * HALF + i * PIECE, PIECE), PIECE)
 
     sent = []
 
@@ -313,71 +325,89 @@
         sent.append(c)
         return c
 
-    first = [go(copy(p_ref.at[piece(1 - core, index(1, d))], rec0.at[d], s0.at[d], t0.at[d], partner)) for d in ORDER + (0,)]
+    swap = {g: go(copy(p.at[1 - core, :, grp[0][g]], rec0.at[g], s0.at[g], t0.at[g], partner)) for g in last_first}
+    loads[1].wait()
     out1 = {}
-    for n, d in enumerate(ORDER + (0,)):
-        first[n].wait_recv()
-        acc0[d] = p_ref[piece(core, index(0, d)), :] + rec0[d]
-        if d:
-            out1[d] = go(copy(acc0.at[d], rec1.at[d - 1], s1.at[d - 1], t1.at[d - 1], peer(0, d)))
-    for d in range(1, 8):
-        out1[d].wait_recv()
-    total = acc0[0]
-    for d in range(1, 8):
-        total = total + rec1[d - 1]
-    acc1[...] = total
+    for g in last_first:
+        swap[g].wait_recv()
+        acc0[g] = p[core, :, grp[1][g]] + rec0[g]
+        for d in FAR_FIRST:
+            out1[g, d] = go(copy(acc0.at[g, idx[d]], rec1.at[g, d - 1], s1.at[g, d - 1], t1.at[g, d - 1], peers[0][d]))
     out2 = {}
-    for e in ORDER:
-        rows = pl.ds(pl.multiple_of(index(1, e) * CH, CH), CH)
-        out2[e] = go(copy(acc1.at[rows], rec2.at[e - 1], s2.at[e - 1], t2.at[e - 1], peer(1, e)))
+    for g in last_first:
+        for d in range(1, 8):
+            out1[g, d].wait_recv()
+        total = acc0[g, idx[0]]
+        for d in range(1, 8):
+            total = total + rec1[g, d - 1]
+        acc1[g] = total
+        for e in (2 * g + 1, 2 * g):
+            if e:
+                out2[e] = go(copy(acc1.at[g, inside(e)], rec2.at[e - 1], s2.at[e - 1], t2.at[e - 1], peers[1][e]))
     for e in range(1, 8):
         out2[e].wait_recv()
-    total = acc1[pl.ds(pl.multiple_of(index(1, 0) * CH, CH), CH), :]
+    total = acc1[0, inside(0), :]
     for e in range(1, 8):
         total = total + rec2[e - 1]
 
     def chunk(e):
-        return pl.ds(pl.multiple_of(core * HALF + index(0, 0) * PIECE + index(1, e) * CH, CH), CH)
-
-    o_ref[chunk(0), :] = total
-    for e in ORDER:
-        go(copy(o_ref.at[chunk(0)], o_ref.at[chunk(0)], s3.at[e - 1], t3.at[e - 1], peer(1, e)))
-    for e in range(1, 8):
-        copy(o_ref.at[chunk(e)], o_ref.at[chunk(e)], s3.at[e - 1], t3.at[e - 1], peer(1, e)).wait_recv()
-    mine = piece(core, index(0, 0))
-    for d in ORDER:
-        go(copy(o_ref.at[mine], o_ref.at[mine], s4.at[d - 1], t4.at[d - 1], peer(0, d)))
-    go(copy(o_ref.at[mine], o_ref.at[mine], s5.at[0], t5.at[0], partner))
-    for d in (1, 2, 4, 3, 5, 6, 7):
-        got = piece(core, index(0, d))
-        copy(o_ref.at[got], o_ref.at[got], s4.at[d - 1], t4.at[d - 1], peer(0, d)).wait_recv()
-        go(copy(o_ref.at[got], o_ref.at[got], s5.at[d], t5.at[d], partner))
-    for d in range(8):
-        got = piece(1 - core, index(1, d))
-        copy(o_ref.at[got], o_ref.at[got], s5.at[d], t5.at[d], partner).wait_recv()
+        return o.at[core, idx[0], grp[1][e // 2], inside(e)]
+
+    o[core, idx[0], grp[1][0], inside(0), :] = total
+    for e in FAR_FIRST:
+        go(copy(chunk(0), chunk(0), s3.at[e - 1], t3.at[e - 1], peers[1][e]))
+    for g in range(4):
+        for e in (2 * g, 2 * g + 1):
+            if e:
+                copy(chunk(e), chunk(e), s3.at[e - 1], t3.at[e - 1], peers[1][e]).wait_recv()
+        for d in FAR_FIRST:
+            mine = o.at[core, idx[0], grp[1][g]]
+            go(copy(mine, mine, s4.at[g, d - 1], t4.at[g, d - 1], peers[0][d]))
+    stores = []
+
+    def store(half, g, n):
+        stores.append(pltpu.make_async_copy(o.at[half, :, g], o_hbm.at[half, :, g], st.at[n]))
+        stores[-1].start()
+
+    for g in range(4):
+        for d in range(1, 8):
+            got = o.at[core, idx[d], grp[1][g]]
+            copy(got, got, s4.at[g, d - 1], t4.at[g, d - 1], peers[0][d]).wait_recv()
+        whole = o.at[core, :, grp[1][g]]
+        go(copy(whole, whole, s5.at[g], t5.at[g], partner))
+        store(core, grp[1][g], g)
+    for g in range(4):
+        got = o.at[1 - core, :, grp[0][g]]
+        copy(got, got, s5.at[g], t5.at[g], partner).wait_recv()
+        store(1 - core, grp[0][g], 4 + g)
     for c in sent:
         c.wait_send()
+    for c in stores:
+        c.wait()
 
 
 def all_reduce(p, ident):
-    sems = []
-    for n in (8, 7, 7, 7, 7, 8):
-        sems += [pltpu.SemaphoreType.DMA((n,))] * 2
+    sems = [pltpu.SemaphoreType.DMA((2,)), pltpu.SemaphoreType.DMA((8,))]
+    for n in ((4,), (4, 7), (7,), (7,), (4, 7), (4,)):
+        sems += [pltpu.SemaphoreType.DMA(n)] * 2
+    buf = lambda *s: pltpu.VMEM(s, jnp.float32)
     return pl.pallas_call(
         ar_kernel,
-        out_shape=jax.ShapeDtypeStruct((ROWS_PACKED, B), jnp.float32),
-        in_specs=[pl.BlockSpec(memory_space=pltpu.VMEM)],
-        out_specs=pl.BlockSpec(memory_space=pltpu.VMEM),
+        out_shape=jax.ShapeDtypeStruct(SUMS, jnp.float32),
+        in_specs=[pl.BlockSpec(memory_space=pl.ANY)],
+        out_specs=pl.BlockSpec(memory_space=pl.ANY),
         scratch_shapes=[
-            pltpu.VMEM((8, PIECE, B), jnp.float32),
-            pltpu.VMEM((8, PIECE, B), jnp.float32),
-            pltpu.VMEM((7, PIECE, B), jnp.float32),
-            pltpu.VMEM((PIECE, B), jnp.float32),
-            pltpu.VMEM((7, CH, B), jnp.float32),
+            buf(*SUMS),
+            buf(*SUMS),
+            buf(4, 8, PAIR, B),
+            buf(4, 8, PAIR, B),
+            buf(4, 7, PAIR, B),
+            buf(4, PAIR, B),
+            buf(7, CH, B),
         ] + sems,
-        compiler_params=pltpu.CompilerParams(collective_id=ident, has_side_effects=True),
+        compiler_params=pltpu.CompilerParams(collective_id=ident, has_side_effects=True, vmem_limit_bytes=40 * 2**20),
         name="sum_group",
-    )(p)
+    )(p.reshape(SUMS)).reshape(ROWS_PACKED, B)
 
 
 def solution(mesh):

time: 203 us -> 194 us (0.956)
  Pallas kernels: 200 us -> 187 us
  local copies, waits for them, and re-layouts: 0 us -> 5.88 us
    pallas_call x2, Pallas kernels: 81.6 us -> 68.4 us  [all_reduce(): pl.pallas_call(ar_kernel, out_shape=jax.ShapeDtypeStruct(SUMS, jnp.float3...]
    unnamed x0 -> x8, local copies, waits for them, and re-layouts: none -> 5.88 us
where the time goes in v4:
time: 194 us
  Pallas kernels  187 us (96%)
  local copies, waits for them, and re-layouts  5.88 us (3%)
    pallas_call x2, Pallas kernels, all_reduce(): pl.pallas_call(ar_kernel, out_shape=jax.ShapeDtypeStruct(SUMS, jnp.float3...  68.4 us
    pallas_call x1, Pallas kernels, sweep_one(): pl.pallas_call(sweep_one_kernel, out_shape=[out(M_LOC, N), out(ROWS_PACKE...  55.7 us
    pallas_call x1, Pallas kernels, sweep_two(): pl.pallas_call(sweep_two_kernel, out_shape=[out(M_LOC, N), out(N, N)], in...  51.1 us
    pallas_call x1, Pallas kernels, gram(): pl.pallas_call(gram_kernel, out_shape=out(ROWS_PACKED, B), in_specs=[ANY]...  11.6 us
    unnamed x8, local copies, waits for them, and re-layouts  5.88 us

profile of v4, /device:TPU:1, one launch (start us, length us, event | category | flops | bytes accessed | tf_op | source)
XLA Modules:
  0.0 193.6 jit_solution(6053019396865957785)
XLA Ops:
  0.6 11.6 %gram.1 = f32[4096,128]{1,0:T(8,128)} custom-call(f32[1024,896]{1,0:T(8,128)} %a_hbm.3), custom_call_target="tpu_custom_call" | custom-call | tf_op jit(solution)/shard_map/gram/pallas_call | solution.py:239
  12.2 0.0 copy-start.2
  12.2 1.6 copy-done.2
  13.8 37.6 %sum_group.2 = f32[2,8,4,64,128]{4,3,2,1,0:T(8,128)S(1)} custom-call(f32[2,8,4,64,128]{4,3,2,1,0:T(8,128)S(1)} %bitcast.6), custom_call_target="tpu_custom_call" | custom-call | tf_op jit(solution)/shard_map/sum_group/pallas_call | solution.py:394
  51.5 0.0 copy-start.1
  51.5 1.3 copy-done.1
  52.8 55.7 %sweep_one.1 = (f32[1024,896]{1,0:T(8,128)}, f32[4096,128]{1,0:T(8,128)}, f32[896,896]{1,0:T(8,128)}) custom-call(f32[4096,128]{1,0:T(8,128)} %bitcast.5, f32[1024,896]{1,0:T(8,128)} %a_hbm.3), custom_call_target="tpu_custom_call" | custom-call | tf_op jit(solution)/shard_map/sweep_one/pallas_call | solution.py:246
  108.5 0.0 copy-start.3
  108.5 1.6 copy-done.3
  110.1 30.8 %sum_group.3 = f32[2,8,4,64,128]{4,3,2,1,0:T(8,128)S(1)} custom-call(f32[2,8,4,64,128]{4,3,2,1,0:T(8,128)S(1)} %bitcast.7), custom_call_target="tpu_custom_call" | custom-call | tf_op jit(solution)/shard_map/sum_group/pallas_call | solution.py:394
  140.9 0.0 copy-start
  140.9 1.4 copy-done
  142.3 51.1 %sweep_two.1 = (f32[1024,896]{1,0:T(8,128)}, f32[896,896]{1,0:T(8,128)}) custom-call(f32[4096,128]{1,0:T(8,128)} %bitcast.4, f32[1024,896]{1,0:T(8,128)} %get-tuple-element.6.a_hbm, f32[896,896]{1,0:T(8,128)} %get-tuple-element.7.r1_hbm), custom_call_target="tpu_custom_call" | custom-call | tf_op jit(solution)/shard_map/sweep_two/pallas_call | solution.py:254
Async XLA Ops:
  12.2 1.6 copy-start.2
  51.5 1.3 copy-start.1
  108.5 1.6 copy-start.3
  140.9 1.4 copy-start

commit v5 on v4

--- a/solution.py
+++ b/solution.py
@@ -30,54 +30,49 @@
     lane = lax.broadcasted_iota(jnp.int32, (8, B), 1)
     m = list(diag)
     rows, inv = [None] * NG, [None] * NG
-    for p in range(NG):
-        g0 = 8 * p
-        here = (lane >= g0) & (lane < g0 + 8)
-        cols = [lane_col(m[p], g0 + k) for k in range(8)]
-        z = jnp.where(here, jnp.where(lane == sub + g0, 1.0, 0.0), m[p])
-        near = p + 1 < NG
-        if near:
-            cq = [lane_col(m[p + 1], g0 + k) for k in range(8)]
-            mq = jnp.where(here, 0.0, m[p + 1])
-        recs = jnp.zeros((8, B), jnp.float32)
-        pivs = jnp.ones((8, B), jnp.float32)
-        for k in range(8):
-            piv = sub_row(cols[k], k)
+    for p in range(NG // 2):
+        g0 = 16 * p
+        here = (lane >= g0) & (lane < g0 + 16)
+        own = m[2 * p:2 * p + 2]
+        cols = [[lane_col(own[r], g0 + k) for k in range(8 * r + 8)] for r in range(2)]
+        dp = list(own)
+        z = [jnp.where(here, jnp.where(lane == sub + (g0 + 8 * r), 1.0, 0.0), own[r]) for r in range(2)]
+        near = m[2 * p + 2:2 * p + 4]
+        cq = [[lane_col(v, g0 + k) for k in range(16)] for v in near]
+        mq = [jnp.where(here, 0.0, v) for v in near]
+        pivs = [jnp.ones((8, B), jnp.float32)] * 2
+        for k in range(16):
+            rk, sk = k // 8, k % 8
+            piv = sub_row(cols[rk][k], sk)
             rec = 1.0 / piv
-            pivs = jnp.where(sub == k, piv, pivs)
-            recs = jnp.where(sub == k, rec, recs)
-            low = jnp.where(sub > k, cols[k] * rec, 0.0)
-            for kk in range(k + 1, 8):
-                cross = sub_row(cols[kk], k)
-                cols[kk] = cols[kk] - low * cross
-                if near:
-                    if kk == k + 1:
-                        lq = cq[k] * rec
-                    cq[kk] = cq[kk] - lq * cross
-            if near and k == 7:
-                lq = cq[k] * rec
-            uz = sub_row(z, k)
-            z = z - low * uz
-            if near:
-                mq = mq - lq * uz
-        scale = lax.rsqrt(pivs)
-        upper = z
-        for kk in range(8):
-            upper = jnp.where(lane == g0 + kk, cols[kk], upper)
-        rows[p] = jnp.where(lane >= sub + g0, upper * scale, 0.0)
-        inv[p] = jnp.where(lane < g0 + 8, z * scale, 0.0)
-        if p + 2 < NG:
-            wv = z * recs
-            for kk in range(7, 0, -1):
-                wv = wv - jnp.where(sub < kk, cols[kk] * recs, 0.0) * sub_row(wv, kk)
-            wk = [sub_row(wv, k) for k in range(8)]
-            for q in range(p + 2, NG):
-                new = jnp.where(here, 0.0, m[q])
-                for k in range(8):
-                    new = new - lane_col(m[q], g0 + k) * wk[k]
-                m[q] = new
-        if near:
-            m[p + 1] = mq
+            pivs[rk] = jnp.where(sub == sk, piv, pivs[rk])
+            for kk in range(k + 1, 16):
+                t = sub_row(cols[kk // 8][k], kk % 8) * rec
+                for r in range(kk // 8, 2):
+                    cols[r][kk] = cols[r][kk] - cols[r][k] * t
+                for c in cq:
+                    c[kk] = c[kk] - c[k] * t
+            v = sub_row(z[rk], sk) * rec
+            y = sub_row(dp[rk], sk) * rec
+            for r in range(rk, 2):
+                low = jnp.where(sub > sk, cols[r][k], 0.0) if r == rk else cols[r][k]
+                z[r] = z[r] - low * v
+                dp[r] = dp[r] - low * y
+            for n, c in enumerate(cq):
+                mq[n] = mq[n] - c[k] * v
+        scaled = []
+        for r in range(2):
+            scale = lax.rsqrt(pivs[r])
+            scaled.append(z[r] * scale)
+            rows[2 * p + r] = jnp.where(lane >= sub + (g0 + 8 * r), dp[r] * scale, 0.0)
+            inv[2 * p + r] = jnp.where(lane < g0 + 16, scaled[r], 0.0)
+        if 2 * p + 4 < NG:
+            both = jnp.concatenate(scaled, axis=0)
+            upd = dot(both, both, 0, 0)
+            for q in range(2 * p + 4, NG):
+                m[q] = jnp.where(here, 0.0, m[q]) - upd[8 * q:8 * q + 8, :]
+        for n, v in enumerate(mq):
+            m[2 * p + 2 + n] = v
     return rows, inv
 
 
@@ -222,7 +217,7 @@
 
 
 VM = pl.BlockSpec(memory_space=pltpu.VMEM)
-ANY = pl.BlockSpec(memory_space=pl.ANY)
+ANY = pl.BlockSpec(memory_space=pltpu.HBM)
 PARAMS = pltpu.CompilerParams(vmem_limit_bytes=58 * 2**20)
 DMA = pltpu.SemaphoreType.DMA
 
@@ -394,8 +389,8 @@
     return pl.pallas_call(
         ar_kernel,
         out_shape=jax.ShapeDtypeStruct(SUMS, jnp.float32),
-        in_specs=[pl.BlockSpec(memory_space=pl.ANY)],
-        out_specs=pl.BlockSpec(memory_space=pl.ANY),
+        in_specs=[pl.BlockSpec(memory_space=pltpu.HBM)],
+        out_specs=pl.BlockSpec(memory_space=pltpu.HBM),
         scratch_shapes=[
             buf(*SUMS),
             buf(*SUMS),
@@ -405,7 +400,7 @@
             buf(4, PAIR, B),
             buf(7, CH, B),
         ] + sems,
-        compiler_params=pltpu.CompilerParams(collective_id=ident, has_side_effects=True, vmem_limit_bytes=40 * 2**20),
+        compiler_params=pltpu.CompilerParams(collective_id=ident, has_side_effects=True, vmem_limit_bytes=63 * 2**20),
         name="sum_group",
     )(p.reshape(SUMS)).reshape(ROWS_PACKED, B)
 

time: 194 us -> 182 us (0.938)
  Pallas kernels: 187 us -> 181 us
  local copies, waits for them, and re-layouts: 5.88 us -> 0 us
    unnamed x8 -> x0, local copies, waits for them, and re-layouts: 5.88 us -> none
    pallas_call x1, Pallas kernels: 55.7 us -> 51.9 us  [sweep_one(): pl.pallas_call(sweep_one_kernel, out_shape=[out(M_LOC, N), out(ROWS_PACKE...]
    pallas_call x1, Pallas kernels: 51.1 us -> 47.3 us  [sweep_two(): pl.pallas_call(sweep_two_kernel, out_shape=[out(M_LOC, N), out(N, N)], in...]
where the time goes in v5:
time: 182 us; the launch traced here: 181 us
  Pallas kernels  181 us (99%)
    pallas_call x2, Pallas kernels, all_reduce(): pl.pallas_call(ar_kernel, out_shape=jax.ShapeDtypeStruct(SUMS, jnp.float3...  69.8 us
    pallas_call x1, Pallas kernels, sweep_one(): pl.pallas_call(sweep_one_kernel, out_shape=[out(M_LOC, N), out(ROWS_PACKE...  51.9 us
    pallas_call x1, Pallas kernels, sweep_two(): pl.pallas_call(sweep_two_kernel, out_shape=[out(M_LOC, N), out(N, N)], in...  47.3 us
    pallas_call x1, Pallas kernels, gram(): pl.pallas_call(gram_kernel, out_shape=out(ROWS_PACKED, B), in_specs=[ANY]...  11.6 us

profile of v5, /device:TPU:1, one launch (start us, length us, event | category | flops | bytes accessed | tf_op | source)
XLA Modules:
  0.0 181.4 jit_solution(862014255235569387)
XLA Ops:
  0.6 11.6 %gram.1 = f32[4096,128]{1,0:T(8,128)} custom-call(f32[1024,896]{1,0:T(8,128)} %a_hbm.3), custom_call_target="tpu_custom_call" | custom-call | tf_op jit(solution)/shard_map/gram/pallas_call | solution.py:234
  12.2 38.1 %sum_group.2 = f32[2,8,4,64,128]{4,3,2,1,0:T(8,128)} custom-call(f32[2,8,4,64,128]{4,3,2,1,0:T(8,128)} %bitcast.6), custom_call_target="tpu_custom_call" | custom-call | tf_op jit(solution)/shard_map/sum_group/pallas_call | solution.py:389
  50.4 51.9 %sweep_one.1 = (f32[1024,896]{1,0:T(8,128)}, f32[4096,128]{1,0:T(8,128)}, f32[896,896]{1,0:T(8,128)}) custom-call(f32[4096,128]{1,0:T(8,128)} %bitcast.5, f32[1024,896]{1,0:T(8,128)} %a_hbm.3), custom_call_target="tpu_custom_call" | custom-call | tf_op jit(solution)/shard_map/sweep_one/pallas_call | solution.py:241
  102.2 31.7 %sum_group.3 = f32[2,8,4,64,128]{4,3,2,1,0:T(8,128)} custom-call(f32[2,8,4,64,128]{4,3,2,1,0:T(8,128)} %bitcast.7), custom_call_target="tpu_custom_call" | custom-call | tf_op jit(solution)/shard_map/sum_group/pallas_call | solution.py:389
  133.9 47.3 %sweep_two.1 = (f32[1024,896]{1,0:T(8,128)}, f32[896,896]{1,0:T(8,128)}) custom-call(f32[4096,128]{1,0:T(8,128)} %bitcast.4, f32[1024,896]{1,0:T(8,128)} %get-tuple-element.6.a_hbm, f32[896,896]{1,0:T(8,128)} %get-tuple-element.7.r1_hbm), custom_call_target="tpu_custom_call" | custom-call | tf_op jit(solution)/shard_map/sweep_two/pallas_call | solution.py:249

commit v6 on v5

v6 whole, which is shorter than its diff:
```python
import jax
import jax.numpy as jnp
from jax import lax
from jax.experimental import pallas as pl
from jax.experimental.pallas import tpu as pltpu
from jax.sharding import PartitionSpec as P

HI = lax.Precision.HIGHEST
N = 896
B = 128
NB = N // B
NG = B // 8


def dot(a, b, ca, cb):
    return lax.dot_general(a, b, (((ca,), (cb,)), ((), ())), precision=HI, preferred_element_type=jnp.float32)


def lane_col(v, c):
    lane = lax.broadcasted_iota(jnp.int32, (8, B), 1)
    return jnp.broadcast_to(jnp.sum(jnp.where(lane == c, v, 0.0), axis=1, keepdims=True), (8, B))


def sub_row(v, k):
    return jnp.broadcast_to(v[k:k + 1, :], (8, B))


def factor_diag(diag):
    sub = lax.broadcasted_iota(jnp.int32, (8, B), 0)
    lane = lax.broadcasted_iota(jnp.int32, (8, B), 1)
    m = list(diag)
    rows, inv = [None] * NG, [None] * NG
    for p in range(NG // 2):
        g0 = 16 * p
        here = (lane >= g0) & (lane < g0 + 16)
        own = m[2 * p:2 * p + 2]
        cols = [[lane_col(own[r], g0 + k) for k in range(8 * r + 8)] for r in range(2)]
        dp = list(own)
        z = [jnp.where(here, jnp.where(lane == sub + (g0 + 8 * r), 1.0, 0.0), own[r]) for r in range(2)]
        near = m[2 * p + 2:2 * p + 4]
        cq = [[lane_col(v, g0 + k) for k in range(16)] for v in near]
        mq = [jnp.where(here, 0.0, v) for v in near]
        pivs = [jnp.ones((8, B), jnp.float32)] * 2
        for k in range(16):
            rk, sk = k // 8, k % 8
            piv = sub_row(cols[rk][k], sk)
            rec = 1.0 / piv
            pivs[rk] = jnp.where(sub == sk, piv, pivs[rk])
            for kk in range(k + 1, 16):
                t = sub_row(cols[kk // 8][k], kk % 8) * rec
                for r in range(kk // 8, 2):
                    cols[r][kk] = cols[r][kk] - cols[r][k] * t
                for c in cq:
                    c[kk] = c[kk] - c[k] * t
            v = sub_row(z[rk], sk) * rec
            y = sub_row(dp[rk], sk) * rec
            for r in range(rk, 2):
                low = jnp.where(sub > sk, cols[r][k], 0.0) if r == rk else cols[r][k]
                z[r] = z[r] - low * v
                dp[r] = dp[r] - low * y
            for n, c in enumerate(cq):
                mq[n] = mq[n] - c[k] * v
        scaled = []
        for r in range(2):
            scale = lax.rsqrt(pivs[r])
            scaled.append(z[r] * scale)
            rows[2 * p + r] = jnp.where(lane >= sub + (g0 + 8 * r), dp[r] * scale, 0.0)
            inv[2 * p + r] = jnp.where(lane < g0 + 16, scaled[r], 0.0)
        if 2 * p + 4 < NG:
            both = jnp.concatenate(scaled, axis=0)
            upd = dot(both, both, 0, 0)
            for q in range(2 * p + 4, NG):
                m[q] = jnp.where(here, 0.0, m[q]) - upd[8 * q:8 * q + 8, :]
        for n, v in enumerate(mq):
            m[2 * p + 2 + n] = v
    return rows, inv


TILES = [(lo, min(lo + 256, N)) for lo in range(0, N, 256)]
TILE_ORDER = (3, 1, 2, 0)
CH = 32
PAIR = 2 * CH
SUMS = (2, 8, 4, PAIR, B)


def _places():
    blocks = [(i, j) for t in TILE_ORDER for j in range(TILES[t][0] // B, TILES[t][1] // B) for i in range(j + 1)]
    return {b: (n % 7 // 4, n % 7 % 4 * 2, n // 7) for n, b in enumerate(blocks)}


PLACE = _places()


def read_block(g_ref, i, j):
    h, m, quarter = PLACE[i, j]
    return g_ref[h, m:m + 2, quarter].reshape(B, B)


def mult(x):
    return pl.multiple_of(x, B)


def factor(g_ref, w, xd):
    w[:, N:] = jnp.zeros((N, N), jnp.float32)
    for i in range(NB):
        for j in range(i):
            w[i * B:(i + 1) * B, j * B:(j + 1) * B] = jnp.zeros((B, B), jnp.float32)
        for j in range(i, NB):
            w[i * B:(i + 1) * B, j * B:(j + 1) * B] = read_block(g_ref, i, j)

    def step(j, _):
        r0 = mult(j * B)
        rr = pl.ds(r0, B)
        group = [pl.ds(pl.multiple_of(r0 + 8 * q, 8), 8) for q in range(NG)]
        rows, inv = factor_diag([w[gq, pl.ds(r0, B)] for gq in group])
        for q in range(NG):
            w[group[q], pl.ds(r0, B)] = rows[q]
            w[group[q], pl.ds(mult(r0 + N), B)] = inv[q]
            xd[pl.ds(8 * q, 8), :] = inv[q]
        mid = pl.ds(mult(r0 + B), N - B)
        w[rr, mid] = dot(xd[...], w[rr, mid], 1, 0)
        odd = j % 2

        def trail(top, depth):
            src = pl.ds(mult(top), depth)
            win = pl.ds(mult(top + depth), N)

            def body(i, _):
                ri = pl.ds(mult(i * B), B)
                w[ri, win] = w[ri, win] - dot(w[src, ri], w[src, win], 0, 0)
                return 0

            return body

        lax.fori_loop(j + 1, jnp.where(odd == 0, jnp.minimum(j + 2, NB), j + 1), trail(r0, B), 0)
        lax.fori_loop(jnp.where(odd == 1, j + 1, NB), NB, trail(jnp.maximum(r0 - B, 0), 2 * B), 0)
        return 0

    lax.fori_loop(0, NB, step, 0)
    for i in range(1, NB):
        w[i * B:(i + 1) * B, :i * B] = jnp.zeros((B, i * B), jnp.float32)


M_LOC = 1024
STEP = 256
NSTEP = M_LOC // STEP


def solve_rows(a, w, q):
    for lo, hi in TILES:
        q[:, lo:hi] = dot(a[:, :hi], w[lo:hi, N:N + hi], 1, 1)


def rows_at(s):
    return pl.ds(pl.multiple_of(s * STEP, STEP), STEP)


MESH_T = pl.DeviceIdType.MESH
FAR_FIRST = (7, 3, 5, 6, 1, 2, 4)


def _bits(d):
    return tuple((d >> s) & 1 for s in range(3))


def _flip(v, kind):
    return (1 - kind) * (v + 1 - 2 * (v % 2)) + kind * (3 - v)


def _label(v, kind):
    return (1 - kind) * ((v % 2 + v // 2) % 2) + kind * (v // 2)


class Net:
    def __init__(self):
        outer, row = lax.axis_index("outer"), lax.axis_index("rows")
        pos = (row // 2, outer % 4, outer // 4)
        self.core = core = row % 2
        kinds = (core, 1 - core)
        labels = [tuple(_label(v, k) for v in pos) for k in kinds]
        self.low = labels[1][0]

        def peer(stage, d):
            x, y, z = (_flip(v, kinds[stage]) if b else v for v, b in zip(pos, _bits(d)))
            return {"outer": z * 4 + y, "rows": x * 2 + core}

        def group(stage, g):
            return sum((1 - labels[stage][s] if (g >> (s - 1)) & 1 else labels[stage][s]) * (1 << (s - 1)) for s in (1, 2))

        self.partner = {"outer": outer, "rows": pos[0] * 2 + 1 - core}
        self.peers = [{d: peer(s, d) for d in range(1, 8)} for s in range(2)]
        self.idx = [sum((1 - v if b else v) * (1 << s) for s, (v, b) in enumerate(zip(labels[0], _bits(d)))) for d in range(8)]
        self.grp = [[group(s, g) for g in range(4)] for s in range(2)]
        self.everyone = [self.partner, *self.peers[0].values(), *self.peers[1].values()]

    def inside(self, e):
        return pl.ds(pl.multiple_of((1 - self.low if e & 1 else self.low) * CH, CH), CH)

    def announce(self):
        for dev in self.everyone:
            pl.semaphore_signal(pltpu.get_barrier_semaphore(), inc=1, device_id=dev, device_id_type=MESH_T)

    def meet(self):
        pl.semaphore_wait(pltpu.get_barrier_semaphore(), len(self.everyone))


def gram_sum(net, a, ready, o_hbm, p, o, rec0, acc0, rec1, acc1, rec2, st, s0, t0, s1, t1, s2, t2, s3, t3, s4, t4, s5, t5):
    core, partner, peers, idx, grp = net.core, net.partner, net.peers, net.idx, net.grp

    def copy(src, dst, send, recv, dev):
        return pltpu.make_async_remote_copy(src_ref=src, dst_ref=dst, send_sem=send, recv_sem=recv, device_id=dev, device_id_type=MESH_T)

    sent = []

    def go(c):
        c.start()
        sent.append(c)
        return c

    def tile(t, wait):
        lo, hi = TILES[t]

        def body(s, _):
            if wait:
                ready(s)
            at = rows_at(s)
            c = dot(a[at, :hi], a[at, lo:hi], 0, 0)
            for j in range(lo // B, hi // B):
                for i in range(j + 1):
                    h, m, quarter = PLACE[i, j]
                    c_ij = c[i * B:(i + 1) * B, j * B - lo:(j + 1) * B - lo]
                    p[h, m:m + 2, quarter] = p[h, m:m + 2, quarter] + c_ij.reshape(2, PAIR, B)
            return 0

        lax.fori_loop(0, NSTEP, body, 0)

    swap = {}

    def exchange(quarter):
        swap[quarter] = go(copy(p.at[1 - core, :, quarter], rec0.at[quarter], s0.at[quarter], t0.at[quarter], partner))

    def out1(quarter, d):
        return copy(acc0.at[quarter, idx[d]], rec1.at[quarter, d - 1], s1.at[quarter, d - 1], t1.at[quarter, d - 1], peers[0][d])

    def scatter(quarter):
        swap[quarter].wait_recv()
        acc0[quarter] = p[core, :, quarter] + rec0[quarter]
        for d in FAR_FIRST:
            go(out1(quarter, d))

    tile(TILE_ORDER[0], True)
    net.meet()
    exchange(0)
    for quarter in range(1, 4):
        tile(TILE_ORDER[quarter], False)
        exchange(quarter)
        scatter(quarter - 1)
    scatter(3)
    out2 = {}
    for g in (3, 2, 1, 0):
        quarter = grp[1][g]
        for d in range(1, 8):
            out1(quarter, d).wait_recv()
        total = acc0[quarter, idx[0]]
        for d in range(1, 8):
            total = total + rec1[quarter, d - 1]
        acc1[g] = total
        for e in (2 * g + 1, 2 * g):
            if e:
                out2[e] = go(copy(acc1.at[g, net.inside(e)], rec2.at[e - 1], s2.at[e - 1], t2.at[e - 1], peers[1][e]))
    for e in range(1, 8):
        out2[e].wait_recv()
    total = acc1[0, net.inside(0), :]
    for e in range(1, 8):
        total = total + rec2[e - 1]

    def chunk(e):
        return o.at[core, idx[0], grp[1][e // 2], net.inside(e)]

    o[core, idx[0], grp[1][0], net.inside(0), :] = total
    for e in FAR_FIRST:
        go(copy(chunk(0), chunk(0), s3.at[e - 1], t3.at[e - 1], peers[1][e]))
    for g in range(4):
        for e in (2 * g, 2 * g + 1):
            if e:
                copy(chunk(e), chunk(e), s3.at[e - 1], t3.at[e - 1], peers[1][e]).wait_recv()
        for d in FAR_FIRST:
            mine = o.at[core, idx[0], grp[1][g]]
            go(copy(mine, mine, s4.at[g, d - 1], t4.at[g, d - 1], peers[0][d]))
    stores = []

    def store(half, g, n):
        stores.append(pltpu.make_async_copy(o.at[half, :, g], o_hbm.at[half, :, g], st.at[n]))
        stores[-1].start()

    for g in range(4):
        for d in range(1, 8):
            got = o.at[core, idx[d], grp[1][g]]
            copy(got, got, s4.at[g, d - 1], t4.at[g, d - 1], peers[0][d]).wait_recv()
        whole = o.at[core, :, grp[1][g]]
        go(copy(whole, whole, s5.at[g], t5.at[g], partner))
        store(core, grp[1][g], g)
    for g in range(4):
        got = o.at[1 - core, :, grp[0][g]]
        copy(got, got, s5.at[g], t5.at[g], partner).wait_recv()
        store(1 - core, grp[0][g], 4 + g)
    for c in sent:
        c.wait_send()
    for c in stores:
        c.wait()


def gram_kernel(a_hbm, o_hbm, a, sem, p, *rest):
    net = Net()
    net.announce()

    def part(s):
        return pltpu.make_async_copy(a_hbm.at[rows_at(s)], a.at[rows_at(s)], sem.at[s])

    for s in range(NSTEP):
        part(s).start()
    p[...] = jnp.zeros(SUMS, jnp.float32)
    gram_sum(net, a, lambda s: part(s).wait(), o_hbm, p, *rest)


def sweep_one_kernel(g_ref, a_hbm, q_hbm, o_hbm, r_hbm, w, xd, a, q, sem, qsem, p, *rest):
    net = Net()
    net.announce()
    load = pltpu.make_async_copy(a_hbm, a, sem.at[0])
    load.start()
    p[...] = jnp.zeros(SUMS, jnp.float32)
    factor(g_ref, w, xd)
    keep = pltpu.make_async_copy(w.at[:, pl.ds(0, N)], r_hbm, sem.at[1])
    keep.start()
    load.wait()

    def part(s):
        return pltpu.make_async_copy(q.at[rows_at(s)], q_hbm.at[rows_at(s)], qsem.at[s])

    def body(s, _):
        solve_rows(a.at[rows_at(s)], w, q.at[rows_at(s)])
        part(s).start()
        return 0

    lax.fori_loop(0, NSTEP, body, 0)
    gram_sum(net, q, lambda s: None, o_hbm, p, *rest)
    for s in range(NSTEP):
        part(s).wait()
    keep.wait()


def sweep_two_kernel(g_ref, a_hbm, r1_hbm, q_hbm, r_hbm, w, xd, a, q, r1, r, sem, qsem, rsem):
    load = pltpu.make_async_copy(a_hbm, a, sem.at[0])
    load.start()
    load_r = pltpu.make_async_copy(r1_hbm, r1, sem.at[1])
    load_r.start()
    factor(g_ref, w, xd)
    load.wait()

    def body(s, _):
        at = rows_at(s)
        solve_rows(a.at[at], w, q.at[at])
        pltpu.make_async_copy(q.at[at], q_hbm.at[at], qsem.at[s]).start()
        return 0

    lax.fori_loop(0, NSTEP, body, 0)
    load_r.wait()
    stores = []
    for n, (lo, hi) in enumerate(TILES):
        if lo:
            r[lo:hi, :lo] = jnp.zeros((hi - lo, lo), jnp.float32)
        for clo, chi in TILES[n:]:
            r[lo:hi, clo:chi] = dot(w[lo:hi, lo:chi], r1[lo:chi, clo:chi], 1, 0)
        at = pl.ds(lo, hi - lo)
        stores.append(pltpu.make_async_copy(r.at[at], r_hbm.at[at], rsem.at[n]))
        stores[-1].start()
    for s in range(NSTEP):
        pltpu.make_async_copy(q.at[rows_at(s)], q_hbm.at[rows_at(s)], qsem.at[s]).wait()
    for c in stores:
        c.wait()


VM = pl.BlockSpec(memory_space=pltpu.VMEM)
ANY = pl.BlockSpec(memory_space=pltpu.HBM)
PARAMS = pltpu.CompilerParams(vmem_limit_bytes=63 * 2**20)
DMA = pltpu.SemaphoreType.DMA


def out(*s):
    return jax.ShapeDtypeStruct(s, jnp.float32)


def buf(*s):
    return pltpu.VMEM(s, jnp.float32)


def sum_scratch():
    sems = [DMA((8,))]
    for n in ((4,), (4, 7), (7,), (7,), (4, 7), (4,)):
        sems += [DMA(n)] * 2
    return [buf(*SUMS), buf(*SUMS), buf(4, 8, PAIR, B), buf(4, 8, PAIR, B), buf(4, 7, PAIR, B), buf(4, PAIR, B), buf(7, CH, B)] + sems


def remote(ident):
    return pltpu.CompilerParams(collective_id=ident, has_side_effects=True, vmem_limit_bytes=63 * 2**20)


def gram(a):
    return pl.pallas_call(
        gram_kernel, out_shape=out(*SUMS), in_specs=[ANY], out_specs=ANY, name="gram",
        scratch_shapes=[buf(M_LOC, N), DMA((NSTEP,))] + sum_scratch(), compiler_params=remote(0),
    )(a)


def sweep_one(g, a):
    return pl.pallas_call(
        sweep_one_kernel, out_shape=[out(M_LOC, N), out(*SUMS), out(N, N)], in_specs=[VM, ANY], out_specs=[ANY, ANY, ANY],
        scratch_shapes=[buf(N, 2 * N), buf(B, B), buf(M_LOC, N), buf(M_LOC, N), DMA((2,)), DMA((NSTEP,))] + sum_scratch(),
        compiler_params=remote(1), name="sweep_one",
    )(g, a)


def sweep_two(g, q1, r1):
    return pl.pallas_call(
        sweep_two_kernel, out_shape=[out(M_LOC, N), out(N, N)], in_specs=[VM, ANY, ANY], out_specs=[ANY, ANY],
        scratch_shapes=[buf(N, 2 * N), buf(B, B), buf(M_LOC, N), buf(M_LOC, N), buf(N, N), buf(N, N), DMA((2,)), DMA((NSTEP,)), DMA((4,))],
        compiler_params=PARAMS, name="sweep_two",
    )(g, q1, r1)


def solution(mesh):
    row_spec = P(("batch", "outer", "rows"), None)

    def local_qr(a):
        q1, g2, r1 = sweep_one(gram(a), a)
        return tuple(sweep_two(g2, q1, r1))

    return jax.shard_map(local_qr, mesh=mesh, in_specs=(row_spec,), out_specs=(row_spec, P("batch", None)), check_vma=False)
```

time: 182 us -> 170 us (0.934)
  Pallas kernels: 181 us -> 169 us
    pallas_call x4 -> x2, Pallas kernels: 133 us -> 121 us  [the longest x1 79.5 us: sweep_one(): pl.pallas_call(sweep_one_kernel, out_shape=[out(M_LOC, N), out(*SUMS), ou...]
where the time goes in v6:
time: 170 us; the launch traced here: 169 us
  Pallas kernels  169 us (99%)
    pallas_call x1, Pallas kernels, sweep_one(): pl.pallas_call(sweep_one_kernel, out_shape=[out(M_LOC, N), out(*SUMS), ou...  79.5 us
    pallas_call x1, Pallas kernels, sweep_two(): pl.pallas_call(sweep_two_kernel, out_shape=[out(M_LOC, N), out(N, N)], in...  47.3 us
    pallas_call x1, Pallas kernels, gram(): pl.pallas_call(gram_kernel, out_shape=out(*SUMS), in_specs=[ANY], out_spe...  41.8 us

profile of v6, /device:TPU:1, one launch (start us, length us, event | category | flops | bytes accessed | tf_op | source)
XLA Modules:
  0.0 169.4 jit_solution(3850706558372374963)
XLA Ops:
  0.6 41.8 %gram.1.g_ref = f32[2,8,4,64,128]{4,3,2,1,0:T(8,128)} custom-call(f32[1024,896]{1,0:T(8,128)} %a_hbm.3), custom_call_target="tpu_custom_call" | custom-call | tf_op jit(solution)/shard_map/gram/pallas_call | solution.py:409
  42.5 79.5 %sweep_one.1 = (f32[1024,896]{1,0:T(8,128)}, f32[2,8,4,64,128]{4,3,2,1,0:T(8,128)}, f32[896,896]{1,0:T(8,128)}) custom-call(f32[2,8,4,64,128]{4,3,2,1,0:T(8,128)} %gram.1.g_ref, f32[1024,896]{1,0:T(8,128)} %a_hbm.3), custom_call_target="tpu_custom_call" | custom-call | tf_op jit(solution)/shard_map/sweep_one/pallas_call | solution.py:416
  122.0 47.3 %sweep_two.1 = (f32[1024,896]{1,0:T(8,128)}, f32[896,896]{1,0:T(8,128)}) custom-call(f32[2,8,4,64,128]{4,3,2,1,0:T(8,128)} %get-tuple-element.5.g_ref, f32[1024,896]{1,0:T(8,128)} %get-tuple-element.6.a_hbm, f32[896,896]{1,0:T(8,128)} %get-tuple-element.7.r1_hbm), custom_call_target="tpu_custom_call" | custom-call | tf_op jit(solution)/shard_map/sweep_two/pallas_call | solution.py:424

commit v7 on v6

--- a/solution.py
+++ b/solution.py
@@ -100,11 +100,14 @@
     return pl.multiple_of(x, B)
 
 
+def clear(w):
+    w[:, N:] = jnp.zeros((N, N), jnp.float32)
+    for i in range(1, NB):
+        w[i * B:(i + 1) * B, :i * B] = jnp.zeros((B, i * B), jnp.float32)
+
+
 def factor(g_ref, w, xd):
-    w[:, N:] = jnp.zeros((N, N), jnp.float32)
     for i in range(NB):
-        for j in range(i):
-            w[i * B:(i + 1) * B, j * B:(j + 1) * B] = jnp.zeros((B, B), jnp.float32)
         for j in range(i, NB):
             w[i * B:(i + 1) * B, j * B:(j + 1) * B] = read_block(g_ref, i, j)
 
@@ -204,7 +207,7 @@
         pl.semaphore_wait(pltpu.get_barrier_semaphore(), len(self.everyone))
 
 
-def gram_sum(net, a, ready, o_hbm, p, o, rec0, acc0, rec1, acc1, rec2, st, s0, t0, s1, t1, s2, t2, s3, t3, s4, t4, s5, t5):
+def gram_sum(net, meet, a, ready, o_hbm, p, o, rec0, acc0, rec1, acc1, rec2, st, s0, t0, s1, t1, s2, t2, s3, t3, s4, t4, s5, t5):
     core, partner, peers, idx, grp = net.core, net.partner, net.peers, net.idx, net.grp
 
     def copy(src, dst, send, recv, dev):
@@ -249,7 +252,7 @@
             go(out1(quarter, d))
 
     tile(TILE_ORDER[0], True)
-    net.meet()
+    meet()
     exchange(0)
     for quarter in range(1, 4):
         tile(TILE_ORDER[quarter], False)
@@ -290,6 +293,8 @@
     stores = []
 
     def store(half, g, n):
+        if o_hbm is None:
+            return
         stores.append(pltpu.make_async_copy(o.at[half, :, g], o_hbm.at[half, :, g], st.at[n]))
         stores[-1].start()
 
@@ -310,51 +315,49 @@
         c.wait()
 
 
-def gram_kernel(a_hbm, o_hbm, a, sem, p, *rest):
+def sweep_one_kernel(a_hbm, q_hbm, o_hbm, r_hbm, w, xd, a, q, asem, qsem, rsem, *sums):
     net = Net()
     net.announce()
-
-    def part(s):
-        return pltpu.make_async_copy(a_hbm.at[rows_at(s)], a.at[rows_at(s)], sem.at[s])
+    first, second = sums[:len(sums) // 2], sums[len(sums) // 2:]
+
+    def a_part(s):
+        return pltpu.make_async_copy(a_hbm.at[rows_at(s)], a.at[rows_at(s)], asem.at[s])
+
+    def q_part(s):
+        return pltpu.make_async_copy(q.at[rows_at(s)], q_hbm.at[rows_at(s)], qsem.at[s])
 
     for s in range(NSTEP):
-        part(s).start()
-    p[...] = jnp.zeros(SUMS, jnp.float32)
-    gram_sum(net, a, lambda s: part(s).wait(), o_hbm, p, *rest)
-
-
-def sweep_one_kernel(g_ref, a_hbm, q_hbm, o_hbm, r_hbm, w, xd, a, q, sem, qsem, p, *rest):
-    net = Net()
-    net.announce()
-    load = pltpu.make_async_copy(a_hbm, a, sem.at[0])
-    load.start()
-    p[...] = jnp.zeros(SUMS, jnp.float32)
-    factor(g_ref, w, xd)
-    keep = pltpu.make_async_copy(w.at[:, pl.ds(0, N)], r_hbm, sem.at[1])
+        a_part(s).start()
+    for p in (first[0], second[0]):
+        p[...] = jnp.zeros(SUMS, jnp.float32)
+    clear(w)
+    gram_sum(net, net.meet, a, lambda s: a_part(s).wait(), None, *first)
+    factor(first[1], w, xd)
+    keep = pltpu.make_async_copy(w.at[:, pl.ds(0, N)], r_hbm, rsem.at[0])
     keep.start()
-    load.wait()
-
-    def part(s):
-        return pltpu.make_async_copy(q.at[rows_at(s)], q_hbm.at[rows_at(s)], qsem.at[s])
 
     def body(s, _):
         solve_rows(a.at[rows_at(s)], w, q.at[rows_at(s)])
-        part(s).start()
+        q_part(s).start()
         return 0
 
     lax.fori_loop(0, NSTEP, body, 0)
-    gram_sum(net, q, lambda s: None, o_hbm, p, *rest)
+    gram_sum(net, lambda: None, q, lambda s: None, o_hbm, *second)
     for s in range(NSTEP):
-        part(s).wait()
+        q_part(s).wait()
     keep.wait()
 
 
-def sweep_two_kernel(g_ref, a_hbm, r1_hbm, q_hbm, r_hbm, w, xd, a, q, r1, r, sem, qsem, rsem):
+def sweep_two_kernel(g_hbm, a_hbm, r1_hbm, q_hbm, r_hbm, g, w, xd, a, q, r1, r, sem, qsem, rsem):
+    load_g = pltpu.make_async_copy(g_hbm, g, sem.at[2])
+    load_g.start()
     load = pltpu.make_async_copy(a_hbm, a, sem.at[0])
     load.start()
     load_r = pltpu.make_async_copy(r1_hbm, r1, sem.at[1])
     load_r.start()
-    factor(g_ref, w, xd)
+    clear(w)
+    load_g.wait()
+    factor(g, w, xd)
     load.wait()
 
     def body(s, _):
@@ -401,29 +404,19 @@
     return [buf(*SUMS), buf(*SUMS), buf(4, 8, PAIR, B), buf(4, 8, PAIR, B), buf(4, 7, PAIR, B), buf(4, PAIR, B), buf(7, CH, B)] + sems
 
 
-def remote(ident):
-    return pltpu.CompilerParams(collective_id=ident, has_side_effects=True, vmem_limit_bytes=63 * 2**20)
-
-
-def gram(a):
+def sweep_one(a):
     return pl.pallas_call(
-        gram_kernel, out_shape=out(*SUMS), in_specs=[ANY], out_specs=ANY, name="gram",
-        scratch_shapes=[buf(M_LOC, N), DMA((NSTEP,))] + sum_scratch(), compiler_params=remote(0),
+        sweep_one_kernel, out_shape=[out(M_LOC, N), out(*SUMS), out(N, N)], in_specs=[ANY], out_specs=[ANY, ANY, ANY],
+        scratch_shapes=[buf(N, 2 * N), buf(B, B), buf(M_LOC, N), buf(M_LOC, N), DMA((NSTEP,)), DMA((NSTEP,)), DMA((1,))]
+        + sum_scratch() + sum_scratch(),
+        compiler_params=pltpu.CompilerParams(collective_id=0, has_side_effects=True, vmem_limit_bytes=63 * 2**20), name="sweep_one",
     )(a)
-
-
-def sweep_one(g, a):
-    return pl.pallas_call(
-        sweep_one_kernel, out_shape=[out(M_LOC, N), out(*SUMS), out(N, N)], in_specs=[VM, ANY], out_specs=[ANY, ANY, ANY],
-        scratch_shapes=[buf(N, 2 * N), buf(B, B), buf(M_LOC, N), buf(M_LOC, N), DMA((2,)), DMA((NSTEP,))] + sum_scratch(),
-        compiler_params=remote(1), name="sweep_one",
-    )(g, a)
 
 
 def sweep_two(g, q1, r1):
     return pl.pallas_call(
-        sweep_two_kernel, out_shape=[out(M_LOC, N), out(N, N)], in_specs=[VM, ANY, ANY], out_specs=[ANY, ANY],
-        scratch_shapes=[buf(N, 2 * N), buf(B, B), buf(M_LOC, N), buf(M_LOC, N), buf(N, N), buf(N, N), DMA((2,)), DMA((NSTEP,)), DMA((4,))],
+        sweep_two_kernel, out_shape=[out(M_LOC, N), out(N, N)], in_specs=[ANY, ANY, ANY], out_specs=[ANY, ANY],
+        scratch_shapes=[buf(*SUMS), buf(N, 2 * N), buf(B, B), buf(M_LOC, N), buf(M_LOC, N), buf(N, N), buf(N, N), DMA((3,)), DMA((NSTEP,)), DMA((4,))],
         compiler_params=PARAMS, name="sweep_two",
     )(g, q1, r1)
 
@@ -432,7 +425,7 @@
     row_spec = P(("batch", "outer", "rows"), None)
 
     def local_qr(a):
-        q1, g2, r1 = sweep_one(gram(a), a)
+        q1, g2, r1 = sweep_one(a)
         return tuple(sweep_two(g2, q1, r1))
 
     return jax.shard_map(local_qr, mesh=mesh, in_specs=(row_spec,), out_specs=(row_spec, P("batch", None)), check_vma=False)

time: 170 us -> 167 us (0.982)
  Pallas kernels: 169 us -> 166 us
    pallas_call x1 -> x0, Pallas kernels: 41.8 us -> none  [gram(): pl.pallas_call(gram_kernel, out_shape=out(*SUMS), in_specs=[ANY], out_spe...]
    pallas_call x1, Pallas kernels: 79.5 us -> 119 us  [sweep_one(): pl.pallas_call(sweep_one_kernel, out_shape=[out(M_LOC, N), out(*SUMS), ou...]
where the time goes in v7:
time: 167 us
  Pallas kernels  166 us (99%)
    pallas_call x1, Pallas kernels, sweep_one(): pl.pallas_call(sweep_one_kernel, out_shape=[out(M_LOC, N), out(*SUMS), ou...  119 us
    pallas_call x1, Pallas kernels, sweep_two(): pl.pallas_call(sweep_two_kernel, out_shape=[out(M_LOC, N), out(N, N)], in...  46.8 us

profile of v7, /device:TPU:1, one launch (start us, length us, event | category | flops | bytes accessed | tf_op | source)
XLA Modules:
  0.0 166.7 jit_solution(17459527708193529148)
XLA Ops:
  0.6 119.1 %sweep_one.1 = (f32[1024,896]{1,0:T(8,128)}, f32[2,8,4,64,128]{4,3,2,1,0:T(8,128)}, f32[896,896]{1,0:T(8,128)}) custom-call(f32[1024,896]{1,0:T(8,128)} %a_hbm.1), custom_call_target="tpu_custom_call" | custom-call | tf_op jit(solution)/shard_map/sweep_one/pallas_call | solution.py:408
  119.8 46.8 %sweep_two.1 = (f32[1024,896]{1,0:T(8,128)}, f32[896,896]{1,0:T(8,128)}) custom-call(f32[2,8,4,64,128]{4,3,2,1,0:T(8,128)} %get-tuple-element.5.g_hbm, f32[1024,896]{1,0:T(8,128)} %get-tuple-element.6.a_hbm, f32[896,896]{1,0:T(8,128)} %get-tuple-element.7.r1_hbm), custom_call_target="tpu_custom_call" | custom-call | tf_op jit(solution)/shard_map/sweep_two/pallas_call | solution.py:417

commit v8 on v7

--- a/solution.py
+++ b/solution.py
@@ -124,19 +124,21 @@
         w[rr, mid] = dot(xd[...], w[rr, mid], 1, 0)
         odd = j % 2
 
-        def trail(top, depth):
+        def trail(top, depth, first, count):
             src = pl.ds(mult(top), depth)
             win = pl.ds(mult(top + depth), N)
 
             def body(i, _):
-                ri = pl.ds(mult(i * B), B)
+                ri = pl.ds(mult((first + count * i) * B), count * B)
                 w[ri, win] = w[ri, win] - dot(w[src, ri], w[src, win], 0, 0)
                 return 0
 
             return body
 
-        lax.fori_loop(j + 1, jnp.where(odd == 0, jnp.minimum(j + 2, NB), j + 1), trail(r0, B), 0)
-        lax.fori_loop(jnp.where(odd == 1, j + 1, NB), NB, trail(jnp.maximum(r0 - B, 0), 2 * B), 0)
+        lax.fori_loop(0, jnp.where(odd == 0, jnp.minimum(NB - 1 - j, 1), 0), trail(r0, B, j + 1, 1), 0)
+        before = jnp.maximum(r0 - B, 0)
+        lax.fori_loop(0, odd, trail(before, 2 * B, j + 1, 1), 0)
+        lax.fori_loop(0, jnp.where(odd == 1, (NB - 2 - j) // 2, 0), trail(before, 2 * B, j + 2, 2), 0)
         return 0
 
     lax.fori_loop(0, NB, step, 0)

time: 167 us -> 165 us (0.988)
  no operation moved by 1% of the time
where the time goes in v8:
time: 165 us
  Pallas kernels  165 us (100%)
    pallas_call x1, Pallas kernels, sweep_one(): pl.pallas_call(sweep_one_kernel, out_shape=[out(M_LOC, N), out(*SUMS), ou...  118 us
    pallas_call x1, Pallas kernels, sweep_two(): pl.pallas_call(sweep_two_kernel, out_shape=[out(M_LOC, N), out(N, N)], in...  46.4 us

profile of v8, /device:TPU:1, one launch (start us, length us, event | category | flops | bytes accessed | tf_op | source)
XLA Modules:
  0.0 165.4 jit_solution(2674403629698987721)
XLA Ops:
  0.6 118.2 %sweep_one.1 = (f32[1024,896]{1,0:T(8,128)}, f32[2,8,4,64,128]{4,3,2,1,0:T(8,128)}, f32[896,896]{1,0:T(8,128)}) custom-call(f32[1024,896]{1,0:T(8,128)} %a_hbm.1), custom_call_target="tpu_custom_call" | custom-call | tf_op jit(solution)/shard_map/sweep_one/pallas_call | solution.py:410
  118.8 46.4 %sweep_two.1 = (f32[1024,896]{1,0:T(8,128)}, f32[896,896]{1,0:T(8,128)}) custom-call(f32[2,8,4,64,128]{4,3,2,1,0:T(8,128)} %get-tuple-element.5.g_hbm, f32[1024,896]{1,0:T(8,128)} %get-tuple-element.6.a_hbm, f32[896,896]{1,0:T(8,128)} %get-tuple-element.7.r1_hbm), custom_call_target="tpu_custom_call" | custom-call | tf_op jit(solution)/shard_map/sweep_two/pallas_call | solution.py:419

commit v9 on v8

--- a/solution.py
+++ b/solution.py
@@ -183,23 +183,16 @@
         self.core = core = row % 2
         kinds = (core, 1 - core)
         labels = [tuple(_label(v, k) for v in pos) for k in kinds]
-        self.low = labels[1][0]
+        self.own = sum(v * (1 << s) for s, v in enumerate(labels[1]))
 
         def peer(stage, d):
             x, y, z = (_flip(v, kinds[stage]) if b else v for v, b in zip(pos, _bits(d)))
             return {"outer": z * 4 + y, "rows": x * 2 + core}
 
-        def group(stage, g):
-            return sum((1 - labels[stage][s] if (g >> (s - 1)) & 1 else labels[stage][s]) * (1 << (s - 1)) for s in (1, 2))
-
         self.partner = {"outer": outer, "rows": pos[0] * 2 + 1 - core}
         self.peers = [{d: peer(s, d) for d in range(1, 8)} for s in range(2)]
         self.idx = [sum((1 - v if b else v) * (1 << s) for s, (v, b) in enumerate(zip(labels[0], _bits(d)))) for d in range(8)]
-        self.grp = [[group(s, g) for g in range(4)] for s in range(2)]
         self.everyone = [self.partner, *self.peers[0].values(), *self.peers[1].values()]
-
-    def inside(self, e):
-        return pl.ds(pl.multiple_of((1 - self.low if e & 1 else self.low) * CH, CH), CH)
 
     def announce(self):
         for dev in self.everyone:
@@ -209,8 +202,8 @@
         pl.semaphore_wait(pltpu.get_barrier_semaphore(), len(self.everyone))
 
 
-def gram_sum(net, meet, a, ready, o_hbm, p, o, rec0, acc0, rec1, acc1, rec2, st, s0, t0, s1, t1, s2, t2, s3, t3, s4, t4, s5, t5):
-    core, partner, peers, idx, grp = net.core, net.partner, net.peers, net.idx, net.grp
+def gram_sum(net, meet, a, ready, o_hbm, p, o, rec0, acc0, rec1, rec2, st, s0, t0, s1, t1, s2, t2, s3, t3, s4, t4):
+    core, partner, peers, idx = net.core, net.partner, net.peers, net.idx
 
     def copy(src, dst, send, recv, dev):
         return pltpu.make_async_remote_copy(src_ref=src, dst_ref=dst, send_sem=send, recv_sem=recv, device_id=dev, device_id_type=MESH_T)
@@ -261,56 +254,67 @@
         exchange(quarter)
         scatter(quarter - 1)
     scatter(3)
-    out2 = {}
-    for g in (3, 2, 1, 0):
-        quarter = grp[1][g]
+    here = net.own
+
+    def out2(quarter, e):
+        return copy(rec2.at[quarter, here], rec2.at[quarter, here], s2.at[quarter, e - 1], t2.at[quarter, e - 1], peers[1][e])
+
+    def spread(quarter):
         for d in range(1, 8):
             out1(quarter, d).wait_recv()
         total = acc0[quarter, idx[0]]
         for d in range(1, 8):
             total = total + rec1[quarter, d - 1]
-        acc1[g] = total
-        for e in (2 * g + 1, 2 * g):
-            if e:
-                out2[e] = go(copy(acc1.at[g, net.inside(e)], rec2.at[e - 1], s2.at[e - 1], t2.at[e - 1], peers[1][e]))
-    for e in range(1, 8):
-        out2[e].wait_recv()
-    total = acc1[0, net.inside(0), :]
-    for e in range(1, 8):
-        total = total + rec2[e - 1]
-
-    def chunk(e):
-        return o.at[core, idx[0], grp[1][e // 2], net.inside(e)]
-
-    o[core, idx[0], grp[1][0], net.inside(0), :] = total
-    for e in FAR_FIRST:
-        go(copy(chunk(0), chunk(0), s3.at[e - 1], t3.at[e - 1], peers[1][e]))
-    for g in range(4):
-        for e in (2 * g, 2 * g + 1):
-            if e:
-                copy(chunk(e), chunk(e), s3.at[e - 1], t3.at[e - 1], peers[1][e]).wait_recv()
+        rec2[quarter, here] = total
+        for e in FAR_FIRST:
+            go(out2(quarter, e))
+
+    def back(quarter, d, owner):
+        at = o.at[core, owner, quarter]
+        return copy(at, at, s3.at[quarter, d - 1], t3.at[quarter, d - 1], peers[0][d])
+
+    def finish(quarter):
+        for e in range(1, 8):
+            out2(quarter, e).wait_recv()
+        total = rec2[quarter, 0]
+        for n in range(1, 8):
+            total = total + rec2[quarter, n]
+        o[core, idx[0], quarter] = total
         for d in FAR_FIRST:
-            mine = o.at[core, idx[0], grp[1][g]]
-            go(copy(mine, mine, s4.at[g, d - 1], t4.at[g, d - 1], peers[0][d]))
+            go(back(quarter, d, idx[0]))
+
     stores = []
 
-    def store(half, g, n):
+    def store(half, quarter, n):
         if o_hbm is None:
             return
-        stores.append(pltpu.make_async_copy(o.at[half, :, g], o_hbm.at[half, :, g], st.at[n]))
+        stores.append(pltpu.make_async_copy(o.at[half, :, quarter], o_hbm.at[half, :, quarter], st.at[n]))
         stores[-1].start()
 
-    for g in range(4):
+    def over(half, quarter):
+        at = o.at[half, :, quarter]
+        return copy(at, at, s4.at[quarter], t4.at[quarter], partner)
+
+    def gather(quarter):
         for d in range(1, 8):
-            got = o.at[core, idx[d], grp[1][g]]
-            copy(got, got, s4.at[g, d - 1], t4.at[g, d - 1], peers[0][d]).wait_recv()
-        whole = o.at[core, :, grp[1][g]]
-        go(copy(whole, whole, s5.at[g], t5.at[g], partner))
-        store(core, grp[1][g], g)
-    for g in range(4):
-        got = o.at[1 - core, :, grp[0][g]]
-        copy(got, got, s5.at[g], t5.at[g], partner).wait_recv()
-        store(1 - core, grp[0][g], 4 + g)
+            back(quarter, d, idx[d]).wait_recv()
+        go(over(core, quarter))
+        store(core, quarter, quarter)
+
+    spread(0)
+    spread(1)
+    spread(2)
+    finish(0)
+    spread(3)
+    finish(1)
+    finish(2)
+    gather(0)
+    finish(3)
+    for quarter in range(1, 4):
+        gather(quarter)
+    for quarter in range(4):
+        over(1 - core, quarter).wait_recv()
+        store(1 - core, quarter, 4 + quarter)
     for c in sent:
         c.wait_send()
     for c in stores:
@@ -401,9 +405,9 @@
 
 def sum_scratch():
     sems = [DMA((8,))]
-    for n in ((4,), (4, 7), (7,), (7,), (4, 7), (4,)):
+    for n in ((4,), (4, 7), (4, 7), (4, 7), (4,)):
         sems += [DMA(n)] * 2
-    return [buf(*SUMS), buf(*SUMS), buf(4, 8, PAIR, B), buf(4, 8, PAIR, B), buf(4, 7, PAIR, B), buf(4, PAIR, B), buf(7, CH, B)] + sems
+    return [buf(*SUMS), buf(*SUMS), buf(4, 8, PAIR, B), buf(4, 8, PAIR, B), buf(4, 7, PAIR, B), buf(4, 8, PAIR, B)] + sems
 
 
 def sweep_one(a):

time: 165 us -> 163 us (0.988)
  Pallas kernels: 165 us -> 162 us
    pallas_call x1, Pallas kernels: 118 us -> 116 us  [sweep_one(): pl.pallas_call(sweep_one_kernel, out_shape=[out(M_LOC, N), out(*SUMS), ou...]
where the time goes in v9:
time: 163 us
  Pallas kernels  162 us (99%)
    pallas_call x1, Pallas kernels, sweep_one(): pl.pallas_call(sweep_one_kernel, out_shape=[out(M_LOC, N), out(*SUMS), ou...  116 us
    pallas_call x1, Pallas kernels, sweep_two(): pl.pallas_call(sweep_two_kernel, out_shape=[out(M_LOC, N), out(N, N)], in...  46.4 us

profile of v9, /device:TPU:1, one launch (start us, length us, event | category | flops | bytes accessed | tf_op | source)
XLA Modules:
  0.0 162.9 jit_solution(5152624562468874191)
XLA Ops:
  0.6 115.7 %sweep_one.1 = (f32[1024,896]{1,0:T(8,128)}, f32[2,8,4,64,128]{4,3,2,1,0:T(8,128)}, f32[896,896]{1,0:T(8,128)}) custom-call(f32[1024,896]{1,0:T(8,128)} %a_hbm.1), custom_call_target="tpu_custom_call" | custom-call | tf_op jit(solution)/shard_map/sweep_one/pallas_call | solution.py:414
  116.3 46.4 %sweep_two.1 = (f32[1024,896]{1,0:T(8,128)}, f32[896,896]{1,0:T(8,128)}) custom-call(f32[2,8,4,64,128]{4,3,2,1,0:T(8,128)} %get-tuple-element.5.g_hbm, f32[1024,896]{1,0:T(8,128)} %get-tuple-element.6.a_hbm, f32[896,896]{1,0:T(8,128)} %get-tuple-element.7.r1_hbm), custom_call_target="tpu_custom_call" | custom-call | tf_op jit(solution)/shard_map/sweep_two/pallas_call | solution.py:423
